TPU v7x, 8 devices: a whole 2x2x1 slice. The times are simulated.
8 devices in a mesh: dp: 2 (over z, y), cp: 4 (over x, core).
Axes of the slice: x: 2, y: 2, z: 1, core: 2. Of those that a mesh axis runs over, the one named last changes fastest.
Arguments:
- x_in: bfloat16 [24, 768, 2048], P('dp', 'cp'), parts along dimension 0
- dy_in: bfloat16 [24, 768, 2048], P('dp', 'cp'), parts along dimension 0
- norm_gain: bfloat16 [2048], replicated
- w_q: bfloat16 [2048, 16, 128], replicated
- w_k: bfloat16 [2048, 2, 128], replicated
- w_v: bfloat16 [2048, 2, 128], replicated
- w_o: bfloat16 [16, 128, 2048], replicated
Outputs:
- output 1: bfloat16 [24, 768, 2048], P('dp', 'cp'), parts along dimension 0
- output 2: bfloat16 [24, 768, 2048], P('dp', 'cp'), parts along dimension 0
- output 3: float32 [4096], P('dp'), parts along dimension 0
- output 4: float32 [4096, 16, 128], P('dp'), parts along dimension 0
- output 5: float32 [4096, 2, 128], P('dp'), parts along dimension 0
- output 6: float32 [4096, 2, 128], P('dp'), parts along dimension 0
- output 7: float32 [32, 128, 2048], P('dp'), parts along dimension 0
There are 2 independent parts. A program takes and returns all parts, laid end to end along the dimension named above; an argument that names none is the same for every part.
All inputs are finite; a program needn't handle non-finite values.
Results may differ from a plain program's by a relative error of at most 0.0101.
Values are sent between devices in bfloat16 or wider.
A program may use at most 1 GiB of HBM per device.

v0:
```python
import jax
import jax.numpy as jnp
from jax import lax
from jax.sharding import PartitionSpec as P

EPS = 1e-6


def attend_pair(queries, key_blk, val_blk, soft_stats, visible):
    run_max, run_sum, run_acc = soft_stats
    score_scale = queries.shape[-1] ** -0.5
    scores = jnp.einsum('bqkgd,bskd->bkgqs', queries, key_blk, preferred_element_type=jnp.float32) * score_scale
    if visible is not None:
        scores = jnp.where(visible, scores, -jnp.inf)
    new_max = jnp.maximum(run_max, jnp.max(scores, axis=-1))
    correction = jnp.exp(run_max - new_max)
    probs_raw = jnp.exp(scores - new_max[..., None])
    run_sum = run_sum * correction + jnp.sum(probs_raw, axis=-1)
    run_acc = run_acc * correction[..., None] + jnp.einsum('bkgqs,bskd->bkgqd', probs_raw.astype(jnp.bfloat16), val_blk, preferred_element_type=jnp.float32)
    return new_max, run_sum, run_acc


def grad_pair(queries, key_blk, val_blk, d_attn, delta_row, log_norm, visible):
    score_scale = queries.shape[-1] ** -0.5
    scores = jnp.einsum('bqkgd,bskd->bkgqs', queries, key_blk, preferred_element_type=jnp.float32) * score_scale
    probs_norm = jnp.exp(scores - log_norm[..., None])
    if visible is not None:
        probs_norm = jnp.where(visible, probs_norm, 0.0)
    d_val = jnp.einsum('bkgqs,bkgqd->bskd', probs_norm.astype(jnp.bfloat16), d_attn, preferred_element_type=jnp.float32)
    d_probs = jnp.einsum('bkgqd,bskd->bkgqs', d_attn, val_blk, preferred_element_type=jnp.float32)
    d_scores = (probs_norm * (d_probs - delta_row[..., None]) * score_scale).astype(jnp.bfloat16)
    d_query = jnp.einsum('bkgqs,bskd->bqkgd', d_scores, key_blk, preferred_element_type=jnp.float32)
    d_key = jnp.einsum('bkgqs,bqkgd->bskd', d_scores, queries, preferred_element_type=jnp.float32)
    return d_query, d_key, d_val


def solution(mesh):
    n_dev = mesh.shape['cp']
    shift_perm = [(src_dev, (src_dev + 1) % n_dev) for src_dev in range(n_dev)]

    def device_fn(x_in, dy_in, norm_gain, w_q, w_k, w_v, w_o):
        my_idx = lax.axis_index('cp')
        n_batch, seq_len, model_dim = x_in.shape
        n_heads, head_dim = w_q.shape[1], w_q.shape[2]
        kv_heads = w_k.shape[1]
        n_group = n_heads // kv_heads
        w_o4 = w_o.reshape(kv_heads, n_group, head_dim, model_dim)
        gain_f32 = norm_gain.astype(jnp.float32)
        x_f32 = x_in.astype(jnp.float32)
        inv_rms = lax.rsqrt(jnp.mean(x_f32 * x_f32, axis=-1, keepdims=True) + EPS)
        unit_x = x_f32 * inv_rms
        x_norm = (unit_x * gain_f32).astype(jnp.bfloat16)
        queries = jnp.einsum('duo,ojf->dujf', x_norm, w_q, preferred_element_type=jnp.float32).astype(jnp.bfloat16).reshape(n_batch, seq_len, kv_heads, n_group, head_dim)
        keys_own = jnp.einsum('bsm,mkd->bskd', x_norm, w_k, preferred_element_type=jnp.float32).astype(jnp.bfloat16)
        vals_own = jnp.einsum('bsm,mkd->bskd', x_norm, w_v, preferred_element_type=jnp.float32).astype(jnp.bfloat16)
        tok_pos = jnp.arange(seq_len)
        causal = tok_pos[:, None] >= tok_pos[None, :]
        stat_shape = (n_batch, kv_heads, n_group, seq_len)
        soft_stats = (jnp.full(stat_shape, -jnp.inf, jnp.float32),
                      jnp.zeros(stat_shape, jnp.float32),
                      jnp.zeros(stat_shape + (head_dim,), jnp.float32))
        soft_stats = attend_pair(queries, keys_own, vals_own, soft_stats, causal)

        def visit_fwd(key_blk, val_blk, stats_in):
            return attend_pair(queries, key_blk, val_blk, stats_in, None)

        def skip_fwd(key_blk, val_blk, stats_in):
            return stats_in

        def fwd_body(step_idx, loop_state):
            key_blk, val_blk, stats_in = loop_state
            key_blk, val_blk = lax.ppermute((key_blk, val_blk), 'cp', shift_perm)
            stats_in = lax.cond(step_idx <= my_idx, visit_fwd, skip_fwd, key_blk, val_blk, stats_in)
            return key_blk, val_blk, stats_in

        fwd_state = lax.fori_loop(1, n_dev, fwd_body, (keys_own, vals_own, soft_stats))
        run_max, run_sum, run_acc = fwd_state[2]
        attn_out = (run_acc / run_sum[..., None]).astype(jnp.bfloat16)
        log_norm = run_max + jnp.log(run_sum)
        proj_out = jnp.einsum('bkgqd,kgdm->bqm', attn_out, w_o4, preferred_element_type=jnp.float32)
        y_out = (x_f32 + proj_out).astype(jnp.bfloat16)

        d_wo = jnp.einsum('bkgqd,bqm->kgdm', attn_out, dy_in, preferred_element_type=jnp.float32).reshape(n_heads, head_dim, model_dim)
        d_attn = jnp.einsum('bqm,kgdm->bkgqd', dy_in, w_o4, preferred_element_type=jnp.float32).astype(jnp.bfloat16)
        delta_row = jnp.einsum('bkgqd,bkgqd->bkgq', d_attn, attn_out, preferred_element_type=jnp.float32)
        d_query, d_key_acc, d_val_acc = grad_pair(queries, keys_own, vals_own, d_attn, delta_row, log_norm, causal)

        def visit_bwd(key_blk, val_blk, grad_acc):
            d_query_c, d_key_c, d_val_c = grad_pair(queries, key_blk, val_blk, d_attn, delta_row, log_norm, None)
            return (grad_acc[0] + d_key_c, grad_acc[1] + d_val_c, grad_acc[2] + d_query_c)

        def skip_bwd(key_blk, val_blk, grad_acc):
            return grad_acc

        def bwd_body(step_idx, loop_state):
            key_blk, val_blk, d_key_blk, d_val_blk, d_query_acc = loop_state
            key_blk, val_blk, d_key_blk, d_val_blk = lax.ppermute((key_blk, val_blk, d_key_blk, d_val_blk), 'cp', shift_perm)
            d_key_blk, d_val_blk, d_query_acc = lax.cond(step_idx <= my_idx, visit_bwd, skip_bwd, key_blk, val_blk, (d_key_blk, d_val_blk, d_query_acc))
            return key_blk, val_blk, d_key_blk, d_val_blk, d_query_acc

        bwd_state = lax.fori_loop(1, n_dev, bwd_body, (keys_own, vals_own, d_key_acc, d_val_acc, d_query))
        d_key_acc, d_val_acc = lax.ppermute((bwd_state[2], bwd_state[3]), 'cp', shift_perm)
        d_query_b = bwd_state[4].astype(jnp.bfloat16).reshape(n_batch, seq_len, n_heads, head_dim)
        d_key_b = d_key_acc.astype(jnp.bfloat16)
        d_val_b = d_val_acc.astype(jnp.bfloat16)
        d_wq = jnp.einsum('duo,dujf->ojf', x_norm, d_query_b, preferred_element_type=jnp.float32)
        d_wk = jnp.einsum('bsm,bskd->mkd', x_norm, d_key_b, preferred_element_type=jnp.float32)
        d_wv = jnp.einsum('bsm,bskd->mkd', x_norm, d_val_b, preferred_element_type=jnp.float32)
        d_norm = (jnp.einsum('dujf,ojf->duo', d_query_b, w_q, preferred_element_type=jnp.float32)
                  + jnp.einsum('bskd,mkd->bsm', d_key_b, w_k, preferred_element_type=jnp.float32)
                  + jnp.einsum('bskd,mkd->bsm', d_val_b, w_v, preferred_element_type=jnp.float32))
        d_gain = jnp.sum(d_norm * unit_x, axis=(0, 1))
        d_unit = d_norm * gain_f32
        dx_out = (dy_in.astype(jnp.float32) + inv_rms * (d_unit - unit_x * jnp.mean(d_unit * unit_x, axis=-1, keepdims=True))).astype(jnp.bfloat16)
        d_gain, d_wq, d_wk, d_wv, d_wo = lax.psum((d_gain, d_wq, d_wk, d_wv, d_wo), 'cp')
        return y_out, dx_out, d_gain, d_wq, d_wk, d_wv, d_wo

    act_spec = P('dp', 'cp', None)
    mat_spec = P(None, None, None)
    grad_spec = P('dp', None, None)
    return jax.shard_map(device_fn, mesh=mesh,
                         in_specs=(act_spec, act_spec, P(None), mat_spec, mat_spec, mat_spec, mat_spec),
                         out_specs=(act_spec, act_spec, P('dp'), grad_spec, grad_spec, grad_spec, grad_spec),
                         check_vma=False)
```

profile of v0, /device:TPU:0, one launch (start us, length us, event | category | flops | bytes accessed | tf_op | source)
XLA Modules:
  0.0 1844.7 jit_solution(9439023625736874157)
XLA Ops:
  7.3 5.7 fusion.43
  13.7 26.1 %fusion.68 = bf16[12,192,16,128]{3,1,2,0:T(8,128)(2,1)} fusion(bf16[2048,16,128]{2,1,0:T(8,128)(2,1)} %param.18, bf16[12,192,2048]{2,1,0:T(8,128)(2,1)} %param.15, f32[2048]{0:T(1024)S(1)} %convert_element_type.78, f32[12,192]{1,0:T(8,128)S(1)} %add_rsqrt_fusion), kind=kOutput, calls=%fused_computation.82 | convolution fusion | flops 19350945792 | bytes 27280384 | tf_op jit(solution)/shard_map/duo,ojf->dujf/dot_general | solution.py:53
  39.8 3.3 convolution_convert_fusion.1
  44.2 26.6 %fusion.28 = (f32[12,2,8,192]{3,2,1,0:T(8,128)S(1)}, f32[12,2,192,192,8]{3,2,4,1,0:T(8,128)}) fusion(pred[192,192]{0,1:T(8,128)(4,1)S(1)} %iota_compare_fusion, bf16[12,192,2,8,128]{4,1,3,2,0:T(8,128)(2,1)} %bitcast.230, bf16[12,192,2,128]{3,1,2,0:T(8,128)(2,1)S(1)} %convolution_convert_fusion.1), kind=kOutput, calls=%fused_computation.36 | convolution fusion | flops 1833136128 | bytes 39112704 | tf_op jit(solution)/shard_map/bqkgd,bskd->bkgqs/dot_general | solution.py:12
  70.8 17.4 fusion.30
  88.3 7.7 convolution_convert_fusion
  98.4 24.0 %broadcast_add_fusion = f32[12,2,8,192,128]{4,3,2,1,0:T(8,128)} fusion(f32[12,2,8,192]{3,2,1,0:T(8,128)S(1)} %get-tuple-element.483, f32[12,2,192,192,8]{3,2,4,1,0:T(8,128)} %get-tuple-element.488, f32[12,2,8,192]{3,2,1,0:T(8,128)S(1)} %get-tuple-element.633, pred[192,192]{0,1:T(8,128)(4,1)S(1)} %iota_compare_fusion, ...), kind=kOutput, calls=%fused_computation.74 | convolution fusion | flops 1844969472 | bytes 48697344 | tf_op jit(solution)/shard_map/bkgqs,bskd->bkgqd/dot_general | solution.py:19
  122.4 226.9 %while.42 = (s32[]{:T(128)}, bf16[12,192,2,128]{3,1,2,0:T(8,128)(2,1)}, bf16[12,192,2,128]{3,1,2,0:T(8,128)(2,1)}, f32[12,2,8,192]{3,2,1,0:T(8,128)S(1)}, f32[12...) while((s32[]{:T(128)}, ...), condition=%wide.region_8.9_spmd, body=%wide.region_3.8_spmd.sunk | while | flops 3690012672 | bytes 150995248 | solution.py:76
  123.4 2.6 collective-permute-start.1
  126.0 13.2 collective-permute-done
  139.2 12.6 collective-permute-done.1
  153.9 69.8 %collective-permute-start = (bf16[12,192,2,128]{3,1,2,0:T(8,128)(2,1)}, bf16[12,192,2,128]{3,1,2,0:T(8,128)(2,1)S(1)}, u32[]{:S(2)}, u32[]{:S(2)}) collective-permute-start(bf16[12,192,2,128]{3,1,2,0:T(8,128)(2,1)} %get-tuple-element.640), channel_id=1, source_target_pairs={{0,1},{1,2},{2,3},{3,0},{4,5},{5,6},{6,7},{7,4}} | collective-permute-start | bytes 3538952 | tf_op jit(solution)/shard_map/while/body/eval_jaxpr/ppermute | solution.py:72
  226.2 10.7 collective-permute-done
  236.9 12.6 collective-permute-done.1
  254.0 72.4 %collective-permute-start.1 = (bf16[12,192,2,128]{3,1,2,0:T(8,128)(2,1)}, bf16[12,192,2,128]{3,1,2,0:T(8,128)(2,1)S(1)}, u32[]{:S(2)}, u32[]{:S(2)}) collective-permute-start(bf16[12,192,2,128]{3,1,2,0:T(8,128)(2,1)} %get-tuple-element.641), channel_id=1, source_target_pairs={{0,1},{1,2},{2,3},{3,0},{4,5},{5,6},{6,7},{7,4}} | collective-permute-start | bytes 3538952 | tf_op jit(solution)/shard_map/while/body/eval_jaxpr/ppermute | solution.py:72
  326.4 8.2 collective-permute-done
  334.6 12.6 collective-permute-done.1
  350.0 28.6 %fusion.107 = (f32[12,2,8,192,128]{4,3,0,2,1:T(8,128)}, bf16[12,2,8,192,128]{4,3,0,2,1:T(8,128)(2,1)}) fusion(bf16[2,8,128,2048,1]{3,2,4,1,0:T(8,128)(2,1)} %bitcast.243, bf16[12,192,2048]{2,1,0:T(8,128)(2,1)} %param.16), kind=kOutput, calls=%fused_computation.120 | convolution fusion | flops 19336790016 | bytes 46137344 | tf_op jit(solution)/shard_map/bqm,kgdm->bkgqd/dot_general | solution.py:84
  378.6 16.0 multiply_reduce_fusion
  394.6 19.7 %fusion.73 = f32[12,192,2,128]{3,1,2,0:T(8,128)} fusion(f32[12,2,192,192,8]{3,2,4,1,0:T(8,128)} %get-tuple-element.488, f32[12,2,8,192]{3,2,1,0:T(8,128)} %log_add_fusion, pred[192,192]{0,1:T(8,128)(4,1)S(1)} %copy-done.11, bf16[12,2,8,192,128]{4,3,0,2,1:T(8,128)(2,1)} %get-tuple-element.486), kind=kOutput, calls=%fused_computation.86 | convolution fusion | flops 1840250880 | bytes 40292352 | tf_op jit(solution)/shard_map/bkgqs,bkgqd->bskd/dot_general | solution.py:29
  414.4 24.0 %multiply_convert_fusion.1 = bf16[12,2,8,192,192]{3,4,2,1,0:T(8,128)(2,1)} fusion(f32[12,2,192,192,8]{3,2,4,1,0:T(8,128)} %get-tuple-element.488, f32[12,2,8,192]{3,2,1,0:T(8,128)} %get-tuple-element.667, f32[12,2,8,192]{3,2,1,0:T(8,128)} %log_add_fusion, pred[192,192]{0,1:T(8,128)(4,1)S(1)} %copy-done.11, ...), kind=kOutput, calls=%fused_computation.34 | convolution fusion | flops 1861484544 | bytes 53415936 | tf_op jit(solution)/shard_map/bkgqd,bskd->bkgqs/dot_general | solution.py:30
  438.4 14.3 convolution_bitcast_fusion
  452.7 14.4 convolution_bitcast_fusion.4
  467.1 10.4 copy.23
  477.4 516.3 %while.43 = (s32[]{:T(128)}, bf16[12,192,2,128]{3,1,2,0:T(8,128)(2,1)S(1)}, bf16[12,192,2,128]{3,1,2,0:T(8,128)(2,1)}, f32[12,192,2,128]{3,1,2,0:T(8,128)}, f32[...) while((s32[]{:T(128)}, ...), condition=%wide.region_12.13_spmd, body=%wide.region_9.12_spmd.sunk | while | flops 9129295872 | bytes 258785712 | solution.py:101
  477.6 4.9 collective-permute-start.4
  485.0 62.3 %collective-permute-start.2 = (bf16[12,192,2,128]{3,1,2,0:T(8,128)(2,1)S(1)}, bf16[12,192,2,128]{3,1,2,0:T(8,128)(2,1)S(1)}, u32[]{:S(2)}, u32[]{:S(2)}) collective-permute-start(bf16[12,192,2,128]{3,1,2,0:T(8,128)(2,1)S(1)} %get-tuple-element.670), channel_id=1, source_target_pairs={{0,1},{1,2},{2,3},{3,0},{4,5},{5,6},{6,7},{7,4}} | collective-permute-start | bytes 3538952 | tf_op jit(solution)/shard_map/while/body/eval_jaxpr/ppermute | solution.py:97
  547.3 63.9 %collective-permute-done.2 = bf16[12,192,2,128]{3,1,2,0:T(8,128)(2,1)S(1)} collective-permute-done((bf16[12,192,2,128]{3,1,2,0:T(8,128)(2,1)S(1)}, bf16[12,192,2,128]{3,1,2,0:T(8,128)(2,1)S(1)}, u32[]{:S(2)}, u32[]{:S(2)}) %collective-permute-start.2) | collective-permute-done | bytes 1179680 | tf_op jit(solution)/shard_map/while/body/eval_jaxpr/ppermute | solution.py:97
  611.3 12.6 collective-permute-done.3
  624.9 3.3 copy.157
  628.2 3.3 copy.158
  631.5 71.4 %collective-permute-start.4 = (f32[12,192,2,128]{3,1,2,0:T(8,128)}, f32[12,192,2,128]{3,1,2,0:T(8,128)}, u32[]{:S(2)}, u32[]{:S(2)}) collective-permute-start(f32[12,192,2,128]{3,1,2,0:T(8,128)} %get-tuple-element.672), channel_id=1, source_target_pairs={{0,1},{1,2},{2,3},{3,0},{4,5},{5,6},{6,7},{7,4}} | collective-permute-start | bytes 7077896 | tf_op jit(solution)/shard_map/while/body/eval_jaxpr/ppermute | solution.py:97
  705.4 22.8 %collective-permute-start.2 = (bf16[12,192,2,128]{3,1,2,0:T(8,128)(2,1)S(1)}, bf16[12,192,2,128]{3,1,2,0:T(8,128)(2,1)S(1)}, u32[]{:S(2)}, u32[]{:S(2)}) collective-permute-start(bf16[12,192,2,128]{3,1,2,0:T(8,128)(2,1)S(1)} %get-tuple-element.670), channel_id=1, source_target_pairs={{0,1},{1,2},{2,3},{3,0},{4,5},{5,6},{6,7},{7,4}} | collective-permute-start | bytes 3538952 | tf_op jit(solution)/shard_map/while/body/eval_jaxpr/ppermute | solution.py:97
  728.2 63.9 %collective-permute-done.2 = bf16[12,192,2,128]{3,1,2,0:T(8,128)(2,1)S(1)} collective-permute-done((bf16[12,192,2,128]{3,1,2,0:T(8,128)(2,1)S(1)}, bf16[12,192,2,128]{3,1,2,0:T(8,128)(2,1)S(1)}, u32[]{:S(2)}, u32[]{:S(2)}) %collective-permute-start.2) | collective-permute-done | bytes 1179680 | tf_op jit(solution)/shard_map/while/body/eval_jaxpr/ppermute | solution.py:97
  792.2 12.6 collective-permute-done.3
  805.8 3.3 copy.157
  809.1 3.3 copy.158
  812.4 76.4 %collective-permute-start.5 = (f32[12,192,2,128]{3,1,2,0:T(8,128)}, f32[12,192,2,128]{3,1,2,0:T(8,128)}, u32[]{:S(2)}, u32[]{:S(2)}) collective-permute-start(f32[12,192,2,128]{3,1,2,0:T(8,128)} %get-tuple-element.673), channel_id=1, source_target_pairs={{0,1},{1,2},{2,3},{3,0},{4,5},{5,6},{6,7},{7,4}} | collective-permute-start | bytes 7077896 | tf_op jit(solution)/shard_map/while/body/eval_jaxpr/ppermute | solution.py:97
  888.8 20.3 %collective-permute-start.2 = (bf16[12,192,2,128]{3,1,2,0:T(8,128)(2,1)S(1)}, bf16[12,192,2,128]{3,1,2,0:T(8,128)(2,1)S(1)}, u32[]{:S(2)}, u32[]{:S(2)}) collective-permute-start(bf16[12,192,2,128]{3,1,2,0:T(8,128)(2,1)S(1)} %get-tuple-element.670), channel_id=1, source_target_pairs={{0,1},{1,2},{2,3},{3,0},{4,5},{5,6},{6,7},{7,4}} | collective-permute-start | bytes 3538952 | tf_op jit(solution)/shard_map/while/body/eval_jaxpr/ppermute | solution.py:97
  909.1 63.9 %collective-permute-done.2 = bf16[12,192,2,128]{3,1,2,0:T(8,128)(2,1)S(1)} collective-permute-done((bf16[12,192,2,128]{3,1,2,0:T(8,128)(2,1)S(1)}, bf16[12,192,2,128]{3,1,2,0:T(8,128)(2,1)S(1)}, u32[]{:S(2)}, u32[]{:S(2)}) %collective-permute-start.2) | collective-permute-done | bytes 1179680 | tf_op jit(solution)/shard_map/while/body/eval_jaxpr/ppermute | solution.py:97
  973.1 12.6 collective-permute-done.3
  986.7 3.3 copy.157
  990.0 3.3 copy.158
  993.7 2.9 convert.12
  996.6 3.0 convert.11
  999.7 7.9 convert_element_type.91
  1007.7 23.8 %convolution_bitcast_fusion.1 = f32[2048,16,128]{2,0,1:T(8,128)} fusion(bf16[12,192,16,128]{3,1,2,0:T(8,128)(2,1)S(1)} %bitcast.241, bf16[12,192,2048]{2,1,0:T(8,128)(2,1)S(1)} %bitcast.235, f32[2048]{0:T(1024)S(1)} %copy-done.16, f32[12,192]{1,0:T(8,128)S(1)} %copy-done.13), kind=kOutput, calls=%fused_computation.83 | convolution fusion | flops 19346227200 | bytes 35668992 | tf_op jit(solution)/shard_map/duo,dujf->ojf/dot_general | solution.py:106
  1031.5 24.7 %fusion.55 = f32[2,8,128,2048,1]{3,2,0,1,4:T(8,128)S(1)} fusion(bf16[12,192,2048]{2,1,0:T(8,128)(2,1)} %param.16, bf16[12,2,8,192,128]{4,3,2,1,0:T(8,128)(2,1)} %get-tuple-element.480), kind=kOutput, calls=%fused_computation.68 | convolution fusion | flops 19327352832 | bytes 35651584 | tf_op jit(solution)/shard_map/bkgqd,bqm->kgdm/dot_general | solution.py:83
  1056.3 6.4 copy.72
  1062.6 44.1 %collective-permute-done.7 = bf16[12,192,2,128]{3,1,2,0:T(8,128)(2,1)} collective-permute-done((bf16[12,192,2,128]{3,1,2,0:T(8,128)(2,1)}, bf16[12,192,2,128]{3,1,2,0:T(8,128)(2,1)}, u32[]{:S(2)}, u32[]{:S(2)}) %collective-permute-start.7) | collective-permute-done | bytes 1179680 | tf_op jit(solution)/shard_map/ppermute | solution.py:102
  1106.7 6.8 convolution_bitcast_fusion.2
  1113.5 5.9 collective-permute-done.6
  1119.3 6.8 convolution_bitcast_fusion.3
  1126.2 26.9 %fusion.62 = f32[12,192,2048,1]{2,1,3,0:T(8,128)} fusion(bf16[12,192,16,128]{3,1,2,0:T(8,128)(2,1)} %bitcast.242, bf16[2048,16,128]{2,1,0:T(8,128)(2,1)} %param.18), kind=kOutput, calls=%fused_computation.76 | convolution fusion | flops 19327352832 | bytes 36700160 | tf_op jit(solution)/shard_map/dujf,ojf->duo/dot_general | solution.py:109
  1153.1 25.7 %fusion.44 = bf16[12,192,2048]{2,1,0:T(8,128)(2,1)} fusion(bf16[12,192,2048]{2,1,0:T(8,128)(2,1)S(1)} %bitcast.237, bf16[12,2,8,192,128]{4,3,2,1,0:T(8,128)(2,1)} %get-tuple-element.480, bf16[2,8,128,2048,1]{3,2,1,0,4:T(8,128)(2,1)} %bitcast.244), kind=kOutput, calls=%fused_computation.55 | convolution fusion | flops 19341508608 | bytes 36700160 | tf_op jit(solution)/shard_map/bkgqd,kgdm->bqm/dot_general | solution.py:80
  1178.8 9.5 fusion.83
  1188.4 24.3 %fusion.42 = (f32[2048]{0:T(1024)S(1)}, f32[12,192]{1,0:T(8,128)S(1)}, f32[12,192,2048]{2,1,0:T(8,128)}) fusion(bf16[12,192,2048]{2,1,0:T(8,128)(2,1)} %param.15, f32[12,192]{1,0:T(8,128)S(1)} %copy-done.14, f32[2048]{0:T(1024)S(1)} %copy-done.17, bf16[12,192,2,128]{3,1,2,0:T(8,128)(2,1)} %collective-permute-done.7, ...), kind=kOutput, calls=%fused_computation.53 | convolution fusion | flops 2458382080 | bytes 68323328 | tf_op jit(solution)/shard_map/bskd,mkd->bsm/dot_general | solution.py:111
  1212.7 53.9 %psum.35 = f32[2048]{0:T(1024)} all-reduce(f32[2048]{0:T(1024)S(1)} %get-tuple-element.433), channel_id=1, replica_groups=mesh['dp'=2,'cp'=4] {'cp'}, use_global_device_ids=true, to_apply=%region_15.16 | all-reduce | flops 2048 | bytes 16384 | tf_op jit(solution)/shard_map/psum | solution.py:115
  1266.6 17.7 fusion.41
  1284.3 510.0 %all-reduce.3.cloned.1.call-done = (f32[2048,16,128]{2,0,1:T(8,128)}, f32[2048,2,128]{2,0,1:T(8,128)}, f32[2048,2,128]{2,0,1:T(8,128)}, f32[16,128,2048]{2,1,0:T(8,128)}) async-done(((f32[2048,16,128]{2,0,1:T(8,128)}, f32[2048,2,128]{2,0,1:T(8,128)}, f32[2048,2,128]{2,0,1:T(8,128)}, f32[16,128,2048]{2,1,0:T(8,128)}), (f32[2048,16,128]{2,0,1:T(8,128)}, f32[2048,2,128]{2,0,1:T(8,128)}, ...) | async-done | bytes 37748752 | tf_op jit(solution)/shard_map/psum | solution.py:115
  1794.3 19.4 %copy.35 = f32[2048,16,128]{2,1,0:T(8,128)} copy(f32[2048,16,128]{2,0,1:T(8,128)} %get-tuple-element.473) | data formatting | bytes 33554432
  1813.8 8.5 copy.36
  1822.3 8.8 copy.37
  1831.2 6.2 copy.166
  (111 shorter events, 25.4 us)
Async XLA Ops:
  7.2 1787.2 %all-reduce.3.cloned.1.call-start = ((), (), s32[]{:S(2)}) async-start(), calls=%async_computation | async-start | bytes 75497472 | tf_op jit(solution)/shard_map/psum | solution.py:115
  7.2 91.2 %copy-start.10 = (pred[192,192]{0,1:T(8,128)(4,1)}, pred[192,192]{0,1:T(8,128)(4,1)S(1)}, u32[]{:S(2)}) copy-start(pred[192,192]{0,1:T(8,128)(4,1)S(1)} %iota_compare_fusion) | copy-start | bytes 110596
  7.3 32.5 %slice-start = ((s8[9437184]{0:T(1024)(128)(4,1)}), s8[1048576]{0:T(1024)(128)(4,1)S(1)}, s32[]{:S(2)}) async-start(s8[9437184]{0:T(1024)(128)(4,1)} %bitcast.232), calls=%async_computation.1 | async-start | bytes 2097152
  13.0 75.3 %copy-start.12 = (f32[12,192]{1,0:T(8,128)}, f32[12,192]{1,0:T(8,128)S(1)}, u32[]{:S(2)}) copy-start(f32[12,192]{1,0:T(8,128)S(1)} %add_rsqrt_fusion) | copy-start | bytes 27652
  13.7 74.6 %copy-start.15 = (f32[2048]{0:T(1024)}, f32[2048]{0:T(1024)S(1)}, u32[]{:S(2)}) copy-start(f32[2048]{0:T(1024)S(1)} %convert_element_type.78) | copy-start | bytes 24580
  13.7 26.1 %slice-start.1 = ((s8[9437184]{0:T(1024)(128)(4,1)}), s8[4194304]{0:T(1024)(128)(4,1)S(1)}, s32[]{:S(2)}) async-start(s8[9437184]{0:T(1024)(128)(4,1)} %bitcast.232), calls=%async_computation.2 | async-start | bytes 8388608
  13.7 26.1 %slice-start.2 = ((s8[9437184]{0:T(1024)(128)(4,1)}), s8[4194304]{0:T(1024)(128)(4,1)S(1)}, s32[]{:S(2)}) async-start(s8[9437184]{0:T(1024)(128)(4,1)} %bitcast.232), calls=%async_computation.3 | async-start | bytes 8388608
  13.7 26.1 %copy-start.8 = (bf16[2048,2,128]{2,1,0:T(2,128)(2,1)S(1)}, bf16[2048,2,128]{2,1,0:T(2,128)(2,1)}, u32[]{:S(2)}) copy-start(bf16[2048,2,128]{2,1,0:T(2,128)(2,1)} %param.19) | copy-start | bytes 3145732
  43.1 53.0 %copy-start.1 = (bf16[12,192,2,128]{3,1,2,0:T(8,128)(2,1)}, bf16[12,192,2,128]{3,1,2,0:T(8,128)(2,1)S(1)}, u32[]{:S(2)}) copy-start(bf16[12,192,2,128]{3,1,2,0:T(8,128)(2,1)S(1)} %convolution_convert_fusion.1) | copy-start | bytes 3538948
  70.8 17.5 copy-start.6
  122.6 16.7 collective-permute-start
  123.4 28.5 %collective-permute-start.1 = (bf16[12,192,2,128]{3,1,2,0:T(8,128)(2,1)}, bf16[12,192,2,128]{3,1,2,0:T(8,128)(2,1)S(1)}, u32[]{:S(2)}, u32[]{:S(2)}) collective-permute-start(bf16[12,192,2,128]{3,1,2,0:T(8,128)(2,1)} %get-tuple-element.641), channel_id=1, source_target_pairs={{0,1},{1,2},{2,3},{3,0},{4,5},{5,6},{6,7},{7,4}} | collective-permute-start | bytes 3538952 | tf_op jit(solution)/shard_map/while/body/eval_jaxpr/ppermute | solution.py:72
  153.9 83.0 %collective-permute-start = (bf16[12,192,2,128]{3,1,2,0:T(8,128)(2,1)}, bf16[12,192,2,128]{3,1,2,0:T(8,128)(2,1)S(1)}, u32[]{:S(2)}, u32[]{:S(2)}) collective-permute-start(bf16[12,192,2,128]{3,1,2,0:T(8,128)(2,1)} %get-tuple-element.640), channel_id=1, source_target_pairs={{0,1},{1,2},{2,3},{3,0},{4,5},{5,6},{6,7},{7,4}} | collective-permute-start | bytes 3538952 | tf_op jit(solution)/shard_map/while/body/eval_jaxpr/ppermute | solution.py:72
  223.7 25.9 %collective-permute-start.1 = (bf16[12,192,2,128]{3,1,2,0:T(8,128)(2,1)}, bf16[12,192,2,128]{3,1,2,0:T(8,128)(2,1)S(1)}, u32[]{:S(2)}, u32[]{:S(2)}) collective-permute-start(bf16[12,192,2,128]{3,1,2,0:T(8,128)(2,1)} %get-tuple-element.641), channel_id=1, source_target_pairs={{0,1},{1,2},{2,3},{3,0},{4,5},{5,6},{6,7},{7,4}} | collective-permute-start | bytes 3538952 | tf_op jit(solution)/shard_map/while/body/eval_jaxpr/ppermute | solution.py:72
  251.6 83.0 %collective-permute-start = (bf16[12,192,2,128]{3,1,2,0:T(8,128)(2,1)}, bf16[12,192,2,128]{3,1,2,0:T(8,128)(2,1)S(1)}, u32[]{:S(2)}, u32[]{:S(2)}) collective-permute-start(bf16[12,192,2,128]{3,1,2,0:T(8,128)(2,1)} %get-tuple-element.640), channel_id=1, source_target_pairs={{0,1},{1,2},{2,3},{3,0},{4,5},{5,6},{6,7},{7,4}} | collective-permute-start | bytes 3538952 | tf_op jit(solution)/shard_map/while/body/eval_jaxpr/ppermute | solution.py:72
  254.0 93.3 %collective-permute-start.1 = (bf16[12,192,2,128]{3,1,2,0:T(8,128)(2,1)}, bf16[12,192,2,128]{3,1,2,0:T(8,128)(2,1)S(1)}, u32[]{:S(2)}, u32[]{:S(2)}) collective-permute-start(bf16[12,192,2,128]{3,1,2,0:T(8,128)(2,1)} %get-tuple-element.641), channel_id=1, source_target_pairs={{0,1},{1,2},{2,3},{3,0},{4,5},{5,6},{6,7},{7,4}} | collective-permute-start | bytes 3538952 | tf_op jit(solution)/shard_map/while/body/eval_jaxpr/ppermute | solution.py:72
  350.0 28.6 %copy-start = (f32[12,2,8,192,128]{4,3,2,1,0:T(8,128)S(1)}, f32[12,2,8,192,128]{4,3,2,1,0:T(8,128)}, u32[]{:S(2)}) copy-start(f32[12,2,8,192,128]{4,3,2,1,0:T(8,128)} %get-tuple-element.409) | copy-start | bytes 56623108
  378.6 16.0 copy-start.11
  414.4 24.0 %copy-start.2 = (bf16[12,192,2,128]{3,1,2,0:T(8,128)(2,1)S(1)}, bf16[12,192,2,128]{3,1,2,0:T(8,128)(2,1)}, u32[]{:S(2)}) copy-start(bf16[12,192,2,128]{3,1,2,0:T(8,128)(2,1)} %copy-done.1) | copy-start | bytes 3538948
  477.6 147.3 %collective-permute-start.4 = (f32[12,192,2,128]{3,1,2,0:T(8,128)}, f32[12,192,2,128]{3,1,2,0:T(8,128)}, u32[]{:S(2)}, u32[]{:S(2)}) collective-permute-start(f32[12,192,2,128]{3,1,2,0:T(8,128)} %get-tuple-element.672), channel_id=1, source_target_pairs={{0,1},{1,2},{2,3},{3,0},{4,5},{5,6},{6,7},{7,4}} | collective-permute-start | bytes 7077896 | tf_op jit(solution)/shard_map/while/body/eval_jaxpr/ppermute | solution.py:97
  482.5 142.3 %collective-permute-start.5 = (f32[12,192,2,128]{3,1,2,0:T(8,128)}, f32[12,192,2,128]{3,1,2,0:T(8,128)}, u32[]{:S(2)}, u32[]{:S(2)}) collective-permute-start(f32[12,192,2,128]{3,1,2,0:T(8,128)} %get-tuple-element.673), channel_id=1, source_target_pairs={{0,1},{1,2},{2,3},{3,0},{4,5},{5,6},{6,7},{7,4}} | collective-permute-start | bytes 7077896 | tf_op jit(solution)/shard_map/while/body/eval_jaxpr/ppermute | solution.py:97
  485.0 126.2 %collective-permute-start.2 = (bf16[12,192,2,128]{3,1,2,0:T(8,128)(2,1)S(1)}, bf16[12,192,2,128]{3,1,2,0:T(8,128)(2,1)S(1)}, u32[]{:S(2)}, u32[]{:S(2)}) collective-permute-start(bf16[12,192,2,128]{3,1,2,0:T(8,128)(2,1)S(1)} %get-tuple-element.670), channel_id=1, source_target_pairs={{0,1},{1,2},{2,3},{3,0},{4,5},{5,6},{6,7},{7,4}} | collective-permute-start | bytes 3538952 | tf_op jit(solution)/shard_map/while/body/eval_jaxpr/ppermute | solution.py:97
  547.3 76.6 %collective-permute-start.3 = (bf16[12,192,2,128]{3,1,2,0:T(8,128)(2,1)}, bf16[12,192,2,128]{3,1,2,0:T(8,128)(2,1)S(1)}, u32[]{:S(2)}, u32[]{:S(2)}) collective-permute-start(bf16[12,192,2,128]{3,1,2,0:T(8,128)(2,1)} %get-tuple-element.671), channel_id=1, source_target_pairs={{0,1},{1,2},{2,3},{3,0},{4,5},{5,6},{6,7},{7,4}} | collective-permute-start | bytes 3538952 | tf_op jit(solution)/shard_map/while/body/eval_jaxpr/ppermute | solution.py:97
  631.5 174.3 %collective-permute-start.4 = (f32[12,192,2,128]{3,1,2,0:T(8,128)}, f32[12,192,2,128]{3,1,2,0:T(8,128)}, u32[]{:S(2)}, u32[]{:S(2)}) collective-permute-start(f32[12,192,2,128]{3,1,2,0:T(8,128)} %get-tuple-element.672), channel_id=1, source_target_pairs={{0,1},{1,2},{2,3},{3,0},{4,5},{5,6},{6,7},{7,4}} | collective-permute-start | bytes 7077896 | tf_op jit(solution)/shard_map/while/body/eval_jaxpr/ppermute | solution.py:97
  702.9 102.9 %collective-permute-start.5 = (f32[12,192,2,128]{3,1,2,0:T(8,128)}, f32[12,192,2,128]{3,1,2,0:T(8,128)}, u32[]{:S(2)}, u32[]{:S(2)}) collective-permute-start(f32[12,192,2,128]{3,1,2,0:T(8,128)} %get-tuple-element.673), channel_id=1, source_target_pairs={{0,1},{1,2},{2,3},{3,0},{4,5},{5,6},{6,7},{7,4}} | collective-permute-start | bytes 7077896 | tf_op jit(solution)/shard_map/while/body/eval_jaxpr/ppermute | solution.py:97
  705.4 86.7 %collective-permute-start.2 = (bf16[12,192,2,128]{3,1,2,0:T(8,128)(2,1)S(1)}, bf16[12,192,2,128]{3,1,2,0:T(8,128)(2,1)S(1)}, u32[]{:S(2)}, u32[]{:S(2)}) collective-permute-start(bf16[12,192,2,128]{3,1,2,0:T(8,128)(2,1)S(1)} %get-tuple-element.670), channel_id=1, source_target_pairs={{0,1},{1,2},{2,3},{3,0},{4,5},{5,6},{6,7},{7,4}} | collective-permute-start | bytes 3538952 | tf_op jit(solution)/shard_map/while/body/eval_jaxpr/ppermute | solution.py:97
  728.2 76.6 %collective-permute-start.3 = (bf16[12,192,2,128]{3,1,2,0:T(8,128)(2,1)}, bf16[12,192,2,128]{3,1,2,0:T(8,128)(2,1)S(1)}, u32[]{:S(2)}, u32[]{:S(2)}) collective-permute-start(bf16[12,192,2,128]{3,1,2,0:T(8,128)(2,1)} %get-tuple-element.671), channel_id=1, source_target_pairs={{0,1},{1,2},{2,3},{3,0},{4,5},{5,6},{6,7},{7,4}} | collective-permute-start | bytes 3538952 | tf_op jit(solution)/shard_map/while/body/eval_jaxpr/ppermute | solution.py:97
  812.4 174.3 %collective-permute-start.4 = (f32[12,192,2,128]{3,1,2,0:T(8,128)}, f32[12,192,2,128]{3,1,2,0:T(8,128)}, u32[]{:S(2)}, u32[]{:S(2)}) collective-permute-start(f32[12,192,2,128]{3,1,2,0:T(8,128)} %get-tuple-element.672), channel_id=1, source_target_pairs={{0,1},{1,2},{2,3},{3,0},{4,5},{5,6},{6,7},{7,4}} | collective-permute-start | bytes 7077896 | tf_op jit(solution)/shard_map/while/body/eval_jaxpr/ppermute | solution.py:97
  812.4 174.3 %collective-permute-start.5 = (f32[12,192,2,128]{3,1,2,0:T(8,128)}, f32[12,192,2,128]{3,1,2,0:T(8,128)}, u32[]{:S(2)}, u32[]{:S(2)}) collective-permute-start(f32[12,192,2,128]{3,1,2,0:T(8,128)} %get-tuple-element.673), channel_id=1, source_target_pairs={{0,1},{1,2},{2,3},{3,0},{4,5},{5,6},{6,7},{7,4}} | collective-permute-start | bytes 7077896 | tf_op jit(solution)/shard_map/while/body/eval_jaxpr/ppermute | solution.py:97
  888.8 84.2 %collective-permute-start.2 = (bf16[12,192,2,128]{3,1,2,0:T(8,128)(2,1)S(1)}, bf16[12,192,2,128]{3,1,2,0:T(8,128)(2,1)S(1)}, u32[]{:S(2)}, u32[]{:S(2)}) collective-permute-start(bf16[12,192,2,128]{3,1,2,0:T(8,128)(2,1)S(1)} %get-tuple-element.670), channel_id=1, source_target_pairs={{0,1},{1,2},{2,3},{3,0},{4,5},{5,6},{6,7},{7,4}} | collective-permute-start | bytes 3538952 | tf_op jit(solution)/shard_map/while/body/eval_jaxpr/ppermute | solution.py:97
  909.1 76.6 %collective-permute-start.3 = (bf16[12,192,2,128]{3,1,2,0:T(8,128)(2,1)}, bf16[12,192,2,128]{3,1,2,0:T(8,128)(2,1)S(1)}, u32[]{:S(2)}, u32[]{:S(2)}) collective-permute-start(bf16[12,192,2,128]{3,1,2,0:T(8,128)(2,1)} %get-tuple-element.671), channel_id=1, source_target_pairs={{0,1},{1,2},{2,3},{3,0},{4,5},{5,6},{6,7},{7,4}} | collective-permute-start | bytes 3538952 | tf_op jit(solution)/shard_map/while/body/eval_jaxpr/ppermute | solution.py:97
  996.6 11.0 slice-start.3
  996.6 11.0 copy-start.13
  996.6 11.0 copy-start.16
  996.6 110.1 %collective-permute-start.7 = (bf16[12,192,2,128]{3,1,2,0:T(8,128)(2,1)}, bf16[12,192,2,128]{3,1,2,0:T(8,128)(2,1)}, u32[]{:S(2)}, u32[]{:S(2)}) collective-permute-start(bf16[12,192,2,128]{3,1,2,0:T(8,128)(2,1)} %convert.12), channel_id=1, source_target_pairs={{0,1},{1,2},{2,3},{3,0},{4,5},{5,6},{6,7},{7,4}} | collective-permute-start | bytes 3538952 | tf_op jit(solution)/shard_map/ppermute | solution.py:102
  999.7 119.6 %collective-permute-start.6 = (bf16[12,192,2,128]{3,1,2,0:T(8,128)(2,1)}, bf16[12,192,2,128]{3,1,2,0:T(8,128)(2,1)}, u32[]{:S(2)}, u32[]{:S(2)}) collective-permute-start(bf16[12,192,2,128]{3,1,2,0:T(8,128)(2,1)} %convert.11), channel_id=1, source_target_pairs={{0,1},{1,2},{2,3},{3,0},{4,5},{5,6},{6,7},{7,4}} | collective-permute-start | bytes 3538952 | tf_op jit(solution)/shard_map/ppermute | solution.py:102
  999.7 8.0 slice-start.4
  999.7 8.0 slice-start.5
  1007.6 23.9 %copy-start.3 = (bf16[12,192,2,8,128]{4,1,3,2,0:T(8,128)(2,1)}, bf16[12,192,2,8,128]{4,1,3,2,0:T(8,128)(2,1)S(1)}, u32[]{:S(2)}) copy-start(bf16[12,192,2,8,128]{4,1,3,2,0:T(8,128)(2,1)S(1)} %convert_element_type.91) | copy-start | bytes 28311556
  1126.1 27.0 %slice-start.6 = ((s8[9437184]{0:T(1024)(128)(4,1)}), s8[1048576]{0:T(1024)(128)(4,1)S(1)}, s32[]{:S(2)}) async-start(s8[9437184]{0:T(1024)(128)(4,1)} %bitcast.236), calls=%async_computation.7 | async-start | bytes 2097152
  1126.1 27.0 %slice-start.7 = ((s8[9437184]{0:T(1024)(128)(4,1)}), s8[4194304]{0:T(1024)(128)(4,1)S(1)}, s32[]{:S(2)}) async-start(s8[9437184]{0:T(1024)(128)(4,1)} %bitcast.236), calls=%async_computation.8 | async-start | bytes 8388608
  1126.1 27.0 %slice-start.8 = ((s8[9437184]{0:T(1024)(128)(4,1)}), s8[4194304]{0:T(1024)(128)(4,1)S(1)}, s32[]{:S(2)}) async-start(s8[9437184]{0:T(1024)(128)(4,1)} %bitcast.236), calls=%async_computation.9 | async-start | bytes 8388608
  1153.1 25.7 %copy-start.9 = (bf16[2048,2,128]{2,1,0:T(2,128)(2,1)S(1)}, bf16[2048,2,128]{2,1,0:T(2,128)(2,1)}, u32[]{:S(2)}) copy-start(bf16[2048,2,128]{2,1,0:T(2,128)(2,1)} %param.19) | copy-start | bytes 3145732
  1178.8 9.5 copy-start.7
  1178.8 9.5 copy-start.14
  1178.8 9.5 copy-start.17
  1794.3 36.8 %slice-start.9 = ((s8[16777216]{0:T(1024)(128)(4,1)}), s8[4194304]{0:T(1024)(128)(4,1)S(1)}, s32[]{:S(2)}) async-start(s8[16777216]{0:T(1024)(128)(4,1)} %bitcast.239), calls=%async_computation.10 | async-start | bytes 8388608
  1794.3 19.5 %copy-start.5 = (f32[2048,2,128]{2,0,1:T(8,128)S(1)}, f32[2048,2,128]{2,0,1:T(8,128)}, u32[]{:S(2)}) copy-start(f32[2048,2,128]{2,0,1:T(8,128)} %get-tuple-element.474) | copy-start | bytes 6291460
  1794.3 28.0 %copy-start.4 = (f32[2048,2,128]{2,0,1:T(8,128)S(1)}, f32[2048,2,128]{2,0,1:T(8,128)}, u32[]{:S(2)}) copy-start(f32[2048,2,128]{2,0,1:T(8,128)} %get-tuple-element.475) | copy-start | bytes 6291460
  1794.3 36.8 %slice-start.10 = ((s8[16777216]{0:T(1024)(128)(4,1)}), s8[4194304]{0:T(1024)(128)(4,1)S(1)}, s32[]{:S(2)}) async-start(s8[16777216]{0:T(1024)(128)(4,1)} %bitcast.239), calls=%async_computation.11 | async-start | bytes 8388608
  1794.3 36.8 %slice-start.11 = ((s8[16777216]{0:T(1024)(128)(4,1)}), s8[4194304]{0:T(1024)(128)(4,1)S(1)}, s32[]{:S(2)}) async-start(s8[16777216]{0:T(1024)(128)(4,1)} %bitcast.239), calls=%async_computation.12 | async-start | bytes 8388608
  1794.3 36.8 %slice-start.12 = ((s8[16777216]{0:T(1024)(128)(4,1)}), s8[4194304]{0:T(1024)(128)(4,1)S(1)}, s32[]{:S(2)}) async-start(s8[16777216]{0:T(1024)(128)(4,1)} %bitcast.239), calls=%async_computation.13 | async-start | bytes 8388608
Sparse Core Ops, SparseCore 0:
  1126.3 668.0 all-reduce.2
where the time goes:
time: 1850 us; the launch traced here: 1840 us
  waiting for transfers between devices  859 us (46%)
  starting transfers between devices  414 us (22%)
  matrix products  337 us (18%)
  local copies, waits for them, and re-layouts  92.5 us (5%)
  other arithmetic  72.1 us (4%)
  blocking collectives  53.9 us (3%)
    psum x1, waiting for transfers between devices, device_fn(): lax.psum((d_gain, d_wq, d_wk, d_wv, d_wo), 'cp')  510 us
    ppermute x12, starting transfers between devices, bwd_body(): lax.ppermute((key_blk, val_blk, d_key_blk, d_val_blk), 'cp', shift_perm)  263 us
    ppermute x12, waiting for transfers between devices, bwd_body(): lax.ppermute((key_blk, val_blk, d_key_blk, d_val_blk), 'cp', shift_perm)  229 us
    ppermute x6, starting transfers between devices, fwd_body(): key_blk, val_blk = lax.ppermute((key_blk, val_blk), 'cp', shift_perm)  151 us
    ppermute x6, waiting for transfers between devices, fwd_body(): key_blk, val_blk = lax.ppermute((key_blk, val_blk), 'cp', shift_perm)  70.1 us
    psum x1, blocking collectives, device_fn(): lax.psum((d_gain, d_wq, d_wk, d_wv, d_wo), 'cp')  53.9 us
    ppermute x2, waiting for transfers between devices, device_fn(): lax.ppermute((bwd_state[2], bwd_state[3]), 'cp', shift_perm)  49.9 us
    unnamed x68, local copies, waits for them, and re-layouts  46.5 us
  transfers between devices with their start and end apart: 21, of which 15 were waited for; matrix products, arithmetic and copies ran while one was open for 10% of the time, Pallas kernels for 0%

commit v1 on v0

v1 whole, which is shorter than its diff:
```python
import functools

import jax
import jax.numpy as jnp
from jax import lax
from jax.experimental import pallas as pl
from jax.experimental.pallas import tpu as pltpu
from jax.sharding import PartitionSpec as P

EPS = 1e-6
F32 = jnp.float32
BF16 = jnp.bfloat16
LOG2E = 1.4426950408889634
MESH = pl.DeviceIdType.MESH
CROSS_AHEAD = 4
PAIR_AHEAD = 2


def dot_nn(a, b):
    return lax.dot_general(a, b, (((1,), (0,)), ((), ())), preferred_element_type=F32)


def dot_nt(a, b):
    return lax.dot_general(a, b, (((1,), (1,)), ((), ())), preferred_element_type=F32)


def group_kernel(xn, dy, wqkv, wo, gx, gy, dwo, dwq, oo, dqo,
                 xb, yb, wq_v, wo_v, acc_o, acc_q, q_s, do_s, k_s, v_s, kt_s, vt_s,
                 ot_s, dqt_s, dk_acc, dv_acc, o_n, dq_n,
                 cs, cr, ds, dr, fs, fr, lsem, wsem, osem, psend, precv, fsem):
    n_seq, blk, dm = xn.shape
    seq = 4 * blk
    n_heads, _, hd = q_s.shape
    qw = n_heads * hd
    half = 2 * blk
    tile = 256
    n_tiles = seq // tile
    c2 = LOG2E * hd ** -0.5
    scale = hd ** -0.5

    me = lax.axis_index('cp')
    core = me % 2
    chip = me // 2
    pair = chip * 2 + (1 - core)
    across = (1 - chip) * 2 + core
    diag = (1 - chip) * 2 + (1 - core)
    src_of = (xn, dy)
    land_of = (gx, gy)
    vmem_of = (xb, yb)

    def cross_copy(t, s):
        return pltpu.make_async_remote_copy(src_of[t].at[s], land_of[t].at[me, s], cs.at[t, s], cr.at[t, s],
                                            device_id={'cp': across}, device_id_type=MESH)

    def cross_arrival(t, s):
        return pltpu.make_async_remote_copy(src_of[t].at[s], land_of[t].at[across, s], cs.at[t, s], cr.at[t, s],
                                            device_id={'cp': across}, device_id_type=MESH)

    def pair_copy(t, s):
        return pltpu.make_async_remote_copy(src_of[t].at[s], land_of[t].at[me, s], ds.at[t, s], dr.at[t, s],
                                            device_id={'cp': pair}, device_id_type=MESH)

    def pair_arrival(t, s):
        return pltpu.make_async_remote_copy(src_of[t].at[s], land_of[t].at[pair, s], ds.at[t, s], dr.at[t, s],
                                            device_id={'cp': pair}, device_id_type=MESH)

    def fwd_copy(t, s):
        return pltpu.make_async_remote_copy(land_of[t].at[across, s], land_of[t].at[across, s], fs.at[t, s], fr.at[t, s],
                                            device_id={'cp': pair}, device_id_type=MESH)

    def fwd_arrival(t, s):
        return pltpu.make_async_remote_copy(land_of[t].at[across, s], land_of[t].at[diag, s], fs.at[t, s], fr.at[t, s],
                                            device_id={'cp': pair}, device_id_type=MESH)

    def rows_of(b):
        return pl.ds(pl.multiple_of(b * blk, 64), blk)

    def load_own(t, s):
        return pltpu.make_async_copy(src_of[t].at[s], vmem_of[t].at[s % 2, rows_of(me)], lsem.at[t, 0])

    def load_from(t, s, b, j):
        return pltpu.make_async_copy(land_of[t].at[b, s], vmem_of[t].at[s % 2, rows_of(b)], lsem.at[t, j])

    def out_copies(s):
        own_rows = pl.ds(pl.multiple_of(core * blk, 64), blk)
        pair_rows = pl.ds(pl.multiple_of((1 - core) * blk, 64), blk)
        res = []
        for idx, (buf, out) in enumerate(((o_n, oo), (dq_n, dqo))):
            width = buf.shape[1]
            cols = pl.ds(pl.multiple_of(core * width, 128), width)
            res.append((pltpu.make_async_copy(buf.at[own_rows], out.at[s, :, cols], osem.at[idx]),
                        pltpu.make_async_remote_copy(buf.at[pair_rows], out.at[s, :, cols], psend.at[idx], precv.at[idx, s],
                                                     device_id={'cp': pair}, device_id_type=MESH)))
        return res

    def out_arrivals(s):
        pair_rows = pl.ds(pl.multiple_of((1 - core) * blk, 64), blk)
        res = []
        for idx, (buf, out) in enumerate(((o_n, oo), (dq_n, dqo))):
            width = buf.shape[1]
            cols = pl.ds(pl.multiple_of((1 - core) * width, 128), width)
            res.append(pltpu.make_async_remote_copy(buf.at[pair_rows], out.at[s, :, cols], psend.at[idx], precv.at[idx, s],
                                                    device_id={'cp': pair}, device_id_type=MESH))
        return res

    load_wq = pltpu.make_async_copy(wqkv, wq_v, wsem.at[0])
    load_wo = pltpu.make_async_copy(wo, wo_v, wsem.at[1])
    load_wq.start()
    load_wo.start()

    barrier = pltpu.get_barrier_semaphore()
    for peer in (pair, across):
        pl.semaphore_signal(barrier, inc=1, device_id={'cp': peer}, device_id_type=MESH)
    pl.semaphore_wait(barrier, 2)

    for s in range(CROSS_AHEAD):
        for t in range(2):
            cross_copy(t, s).start()
            if s < PAIR_AHEAD:
                pair_copy(t, s).start()
    for t in range(2):
        load_own(t, 0).start()
    acc_o[...] = jnp.zeros_like(acc_o)
    acc_q[...] = jnp.zeros_like(acc_q)
    for t in range(2):
        pair_arrival(t, 0).wait_recv()
        load_from(t, 0, pair, 1).start()
    load_wq.wait()
    load_wo.wait()

    def project_x(slot, r0):
        rows = pl.ds(pl.multiple_of(r0, 128), half)
        for n in range((qw + 2 * hd) // tile):
            res = dot_nn(xb[slot, rows, :], wq_v[:, n * tile:(n + 1) * tile]).astype(BF16)
            for part in range(tile // hd):
                col = n * tile + part * hd
                piece = res[:, part * hd:(part + 1) * hd]
                if col < qw:
                    q_s[col // hd, rows, :] = piece
                elif col == qw:
                    k_s[rows, :] = piece
                else:
                    v_s[rows, :] = piece

    def project_dy(slot, r0):
        rows = pl.ds(pl.multiple_of(r0, 128), half)
        for n in range(qw // tile):
            res = dot_nt(yb[slot, rows, :], wo_v[n * tile:(n + 1) * tile, :]).astype(BF16)
            for part in range(tile // hd):
                do_s[(n * tile + part * hd) // hd, rows, :] = res[:, part * hd:(part + 1) * hd]

    def head_step(h, carry):
        hrows = pl.ds(pl.multiple_of(h * hd, hd), hd)
        for i in range(n_tiles):
            nk = (i + 1) * tile
            qi = q_s[h, i * tile:(i + 1) * tile, :]
            doi = do_s[h, i * tile:(i + 1) * tile, :]
            st = dot_nt(k_s[0:nk, :], qi)
            key_pos = lax.broadcasted_iota(jnp.int32, (nk, tile), 0)
            qry_pos = lax.broadcasted_iota(jnp.int32, (nk, tile), 1) + i * tile
            st = jnp.where(key_pos <= qry_pos, st, -jnp.inf)
            mx = jnp.max(st, axis=0, keepdims=True)
            p = jnp.exp2(st * c2 - mx * c2)
            inv_l = 1.0 / jnp.sum(p, axis=0, keepdims=True)
            ot = (dot_nn(vt_s[:, 0:nk], p.astype(BF16)) * inv_l).astype(BF16)
            ot_s[hrows, i * tile:(i + 1) * tile] = ot
            dot_i = doi.astype(F32).T
            delta = jnp.sum(dot_i * ot.astype(F32), axis=0, keepdims=True)
            dpt = dot_nt(v_s[0:nk, :], doi)
            pn = p * inv_l
            dst = (pn * (dpt - delta) * scale).astype(BF16)
            dv_acc[0:nk, :] += dot_nn(pn.astype(BF16), doi)
            dk_acc[0:nk, :] += dot_nn(dst, qi)
            dqt_s[hrows, i * tile:(i + 1) * tile] = dot_nn(kt_s[:, 0:nk], dst).astype(BF16)
        own_cols = pl.ds(pl.multiple_of(chip * half, 128), half)
        hcols = pl.ds(pl.multiple_of(h * hd, hd), hd)
        o_n[:, hcols] = ot_s[hrows, own_cols].T
        dq_n[:, hcols] = dqt_s[hrows, own_cols].T
        return carry

    def seq_step(s, carry):
        slot = s % 2
        @pl.when(s + CROSS_AHEAD < n_seq)
        def _():
            for t in range(2):
                cross_copy(t, s + CROSS_AHEAD).start()
        @pl.when(s + PAIR_AHEAD < n_seq)
        def _():
            for t in range(2):
                pair_copy(t, s + PAIR_AHEAD).start()

        cross_arrival(0, s).wait_recv()
        fwd_copy(0, s).start()
        load_from(0, s, across, 2).start()
        for t in range(2):
            load_own(t, s).wait()
            load_from(t, s, pair, 1).wait()
        near = chip * half
        far = (1 - chip) * half
        project_x(slot, near)
        project_dy(slot, near)
        fwd_arrival(0, s).wait_recv()
        load_from(0, s, diag, 3).start()
        load_from(0, s, across, 2).wait()
        load_from(0, s, diag, 3).wait()
        project_x(slot, far)
        cross_arrival(1, s).wait_recv()
        fwd_copy(1, s).start()
        load_from(1, s, across, 2).start()
        fwd_arrival(1, s).wait_recv()
        load_from(1, s, diag, 3).start()

        kt_s[...] = k_s[...].T
        vt_s[...] = v_s[...].T
        dk_acc[...] = jnp.zeros_like(dk_acc)
        dv_acc[...] = jnp.zeros_like(dv_acc)
        load_from(1, s, across, 2).wait()
        load_from(1, s, diag, 3).wait()
        project_dy(slot, far)

        @pl.when(s + 1 < n_seq)
        def _():
            for t in range(2):
                load_own(t, s + 1).start()
                pair_arrival(t, s + 1).wait_recv()
                load_from(t, s + 1, pair, 1).start()

        @pl.when(s > 0)
        def _():
            for local, remote in out_copies(s - 1):
                local.wait()
                remote.wait_send()

        lax.fori_loop(0, n_heads, head_step, 0)

        near_rows = pl.ds(pl.multiple_of(near, 128), half)
        for idx, acc in enumerate((dk_acc, dv_acc)):
            lo = qw + idx * hd
            dqt_s[lo:lo + hd, :] = acc[...].T.astype(BF16)
            dq_n[:, lo:lo + hd] = acc[near_rows, :].astype(BF16)
        for local, remote in out_copies(s):
            local.start()
            remote.start()

        def dw_step(n, c):
            cols = pl.ds(pl.multiple_of(n * 2 * tile, 2 * tile), 2 * tile)
            acc_o[:, cols] += dot_nn(ot_s[...], yb[slot, :, cols])
            acc_q[:, cols] += dot_nn(dqt_s[...], xb[slot, :, cols])
            return c

        lax.fori_loop(0, dm // (2 * tile), dw_step, 0)
        return carry

    lax.fori_loop(0, n_seq, seq_step, 0)

    flush_o = pltpu.make_async_copy(acc_o, dwo, fsem.at[0])
    flush_q = pltpu.make_async_copy(acc_q, dwq, fsem.at[1])
    flush_o.start()
    flush_q.start()
    for local, remote in out_copies(n_seq - 1):
        local.wait()
        remote.wait_send()

    def drain(s, carry):
        for t in range(2):
            cross_copy(t, s).wait_send()
            pair_copy(t, s).wait_send()
            fwd_copy(t, s).wait_send()
        for arrival in out_arrivals(s):
            arrival.wait_recv()
        return carry

    lax.fori_loop(0, n_seq, drain, 0)
    flush_o.wait()
    flush_q.wait()


def group_call(x_norm, dy_in, wqkv, wo):
    n_seq, blk, dm = x_norm.shape
    seq = 4 * blk
    qw = wo.shape[0]
    hd = (wqkv.shape[1] - qw) // 2
    n_heads = qw // hd
    kw = wqkv.shape[1]
    any_spec = pl.BlockSpec(memory_space=pl.ANY)
    dma = pltpu.SemaphoreType.DMA
    return pl.pallas_call(
        group_kernel,
        out_shape=(
            jax.ShapeDtypeStruct((4, n_seq, blk, dm), BF16),
            jax.ShapeDtypeStruct((4, n_seq, blk, dm), BF16),
            jax.ShapeDtypeStruct((qw, dm), F32),
            jax.ShapeDtypeStruct((kw, dm), F32),
            jax.ShapeDtypeStruct((n_seq, blk, 2 * qw), BF16),
            jax.ShapeDtypeStruct((n_seq, blk, 2 * kw), BF16),
        ),
        in_specs=[any_spec] * 4,
        out_specs=(any_spec,) * 6,
        scratch_shapes=[
            pltpu.VMEM((2, seq, dm), BF16), pltpu.VMEM((2, seq, dm), BF16),
            pltpu.VMEM((dm, kw), BF16), pltpu.VMEM((qw, dm), BF16),
            pltpu.VMEM((qw, dm), F32), pltpu.VMEM((kw, dm), F32),
            pltpu.VMEM((n_heads, seq, hd), BF16), pltpu.VMEM((n_heads, seq, hd), BF16),
            pltpu.VMEM((seq, hd), BF16), pltpu.VMEM((seq, hd), BF16),
            pltpu.VMEM((hd, seq), BF16), pltpu.VMEM((hd, seq), BF16),
            pltpu.VMEM((qw, seq), BF16), pltpu.VMEM((kw, seq), BF16),
            pltpu.VMEM((seq, hd), F32), pltpu.VMEM((seq, hd), F32),
            pltpu.VMEM((2 * blk, qw), BF16), pltpu.VMEM((2 * blk, kw), BF16),
            dma((2, n_seq)), dma((2, n_seq)), dma((2, n_seq)), dma((2, n_seq)), dma((2, n_seq)), dma((2, n_seq)),
            dma((2, 4)), dma((2,)), dma((2,)), dma((2,)), dma((2, n_seq)), dma((2,)),
        ],
        compiler_params=pltpu.CompilerParams(collective_id=0, has_side_effects=True, vmem_limit_bytes=67_000_000),
    )(x_norm, dy_in, wqkv, wo)


def solution(mesh):
    def device_fn(x_in, dy_in, norm_gain, w_q, w_k, w_v, w_o):
        n_batch, blk, dm = x_in.shape
        n_heads, hd = w_q.shape[1], w_q.shape[2]
        kv_heads = w_k.shape[1]
        n_group = n_heads // kv_heads
        core = lax.axis_index('cp') % 2
        gain = norm_gain.astype(F32)
        x_f32 = x_in.astype(F32)
        inv_rms = lax.rsqrt(jnp.mean(x_f32 * x_f32, axis=-1, keepdims=True) + EPS)
        unit = x_f32 * inv_rms
        x_norm = (unit * gain).astype(BF16)

        w_all = jnp.concatenate(
            [part for g in range(kv_heads) for part in
             (w_q[:, g * n_group:(g + 1) * n_group].reshape(dm, n_group * hd), w_k[:, g], w_v[:, g])], axis=1)
        kw = w_all.shape[1] // kv_heads
        wqkv = lax.dynamic_slice(w_all, (0, core * kw), (dm, kw))
        wo_all = w_o.reshape(n_heads * hd, dm)
        wo = lax.dynamic_slice(wo_all, (core * n_group * hd, 0), (n_group * hd, dm))

        _, _, dwo_half, dwq_half, o_own, dq_own = group_call(x_norm, dy_in, wqkv, wo)

        pairs = [[0, 1], [2, 3]]
        d_wo = lax.all_gather(dwo_half, 'cp', axis_index_groups=pairs, tiled=True).reshape(n_heads, hd, dm)
        dwq_all = lax.all_gather(dwq_half, 'cp', axis_index_groups=pairs)
        qw = n_group * hd
        d_wq = dwq_all[:, :qw].reshape(n_heads, hd, dm).transpose(2, 0, 1)
        d_wk = dwq_all[:, qw:qw + hd].transpose(2, 0, 1)
        d_wv = dwq_all[:, qw + hd:].transpose(2, 0, 1)

        y_out = (x_f32 + jnp.einsum('bsf,fm->bsm', o_own, wo_all, preferred_element_type=F32)).astype(BF16)
        d_norm = jnp.einsum('bsf,mf->bsm', dq_own, w_all, preferred_element_type=F32)
        d_gain = lax.psum(jnp.sum(d_norm * unit, axis=(0, 1)), 'cp')
        d_unit = d_norm * gain
        dx_out = (dy_in.astype(F32) + inv_rms * (d_unit - unit * jnp.mean(d_unit * unit, axis=-1, keepdims=True))).astype(BF16)
        return y_out, dx_out, d_gain, d_wq, d_wk, d_wv, d_wo

    act_spec = P('dp', 'cp', None)
    mat_spec = P(None, None, None)
    grad_spec = P('dp', None, None)
    return jax.shard_map(device_fn, mesh=mesh,
                         in_specs=(act_spec, act_spec, P(None), mat_spec, mat_spec, mat_spec, mat_spec),
                         out_specs=(act_spec, act_spec, P('dp'), grad_spec, grad_spec, grad_spec, grad_spec),
                         check_vma=False)
```

time: 1850 us -> 715 us (0.39)
  waiting for transfers between devices: 859 us -> 0.71 us
  Pallas kernels: 0 us -> 516 us
  starting transfers between devices: 414 us -> 0.08 us
  matrix products: 337 us -> 61 us
  blocking collectives: 53.9 us -> 8.81 us
  other arithmetic: 72.1 us -> 34.3 us
    pallas_call x0 -> x1, Pallas kernels: none -> 516 us  [group_call(): pl.pallas_call(group_kernel, out_shape=(jax.ShapeDtypeStruct((4, n_seq, b...]
    psum x1 -> x0, waiting for transfers between devices: 510 us -> none  [device_fn(): lax.psum((d_gain, d_wq, d_wk, d_wv, d_wo), 'cp')]
    ppermute x20 -> x0, starting transfers between devices: 414 us -> none  [the longest x12 263 us: bwd_body(): lax.ppermute((key_blk, val_blk, d_key_blk, d_val_blk), 'cp', shift_perm)]
    ppermute x20 -> x0, waiting for transfers between devices: 349 us -> none  [the longest x12 229 us: bwd_body(): lax.ppermute((key_blk, val_blk, d_key_blk, d_val_blk), 'cp', shift_perm)]
    dot_general x18 -> x2, matrix products: 337 us -> 61 us  [the longest x1 34.1 us: device_fn(): jnp.einsum('bsf,mf->bsm', dq_own, w_all, preferred_element_type=F32)]
    psum x1, blocking collectives: 53.9 us -> 8.81 us  [device_fn(): d_gain = lax.psum(jnp.sum(d_norm * unit, axis=(0, 1)), 'cp')]
    while x18 -> x0, local copies, waits for them, and re-layouts: 29.2 us -> none
    slice x0 -> x5, local copies, waits for them, and re-layouts: none -> 22.6 us  [the longest x1 11.8 us: device_fn(): d_wq = dwq_all[:, :qw].reshape(n_heads, hd, dm).transpose(2, 0, 1)]
  transfers between devices with their start and end apart: 21 -> 2, of which waited for: 15 -> 0; matrix products, arithmetic and copies ran while one was open for 10% -> 11% of each run, Pallas kernels for 0% -> 0%
where the time goes in v1:
time: 715 us; the launch traced here: 713 us
  Pallas kernels  516 us (72%)
  local copies, waits for them, and re-layouts  78.7 us (11%)
  matrix products  61 us (9%)
  other arithmetic  34.3 us (5%)
  between operations  14.1 us (2%)
  blocking collectives  8.81 us (1%)
    pallas_call x1, Pallas kernels, group_call(): pl.pallas_call(group_kernel, out_shape=(jax.ShapeDtypeStruct((4, n_seq, b...  516 us
    dot_general x1, matrix products, device_fn(): jnp.einsum('bsf,mf->bsm', dq_own, w_all, preferred_element_type=F32)  34.1 us
    unnamed x22, local copies, waits for them, and re-layouts  27.5 us
    dot_general x1, matrix products, device_fn(): jnp.einsum('bsf,fm->bsm', o_own, wo_all, preferred_element_type=F32)  26.9 us
    convert_element_type x1, other arithmetic, device_fn(): (dy_in.astype(F32) + inv_rms * (d_unit - unit * jnp.mean(d_unit * unit, a...  17.8 us
    reshape x1, local copies, waits for them, and re-layouts, device_fn(): d_wq = dwq_all[:, :qw].reshape(n_heads, hd, dm).transpose(2, 0, 1)  17.6 us
  transfers between devices with their start and end apart: 2, of which 0 were waited for; matrix products, arithmetic and copies ran while one was open for 11% of the time, Pallas kernels for 0%

profile of v1, /device:TPU:0, one launch (start us, length us, event | category | flops | bytes accessed | tf_op | source)
XLA Modules:
  0.0 713.4 jit_solution(7258862083824197407)
XLA Ops:
  7.2 0.0 copy-start.1
  7.2 0.0 copy-start.2
  7.2 0.0 all-gather.4.cloned.1.call-start
  7.3 0.0 slice-start
  7.3 0.8 convert_element_type.19
  8.1 0.0 slice-start.1
  8.1 6.0 fusion.11
  14.2 0.0 copy-done.1
  14.2 2.3 fusion.22
  16.5 0.0 copy-done.2
  16.5 2.3 fusion.21
  18.7 0.0 slice-done
  18.7 0.0 slice-done.1
  18.7 2.3 fusion.20
  21.0 0.0 copy-start.3
  21.0 3.4 bitcast_dynamic-update-slice_fusion.1
  24.4 0.0 copy-start.4
  24.4 0.0 copy-start
  24.4 4.9 constant_dynamic-slice_fusion.wo
  29.3 0.0 copy-done.3
  29.3 0.9 fusion.18
  30.2 0.0 copy-done.4
  30.2 0.9 fusion.17
  31.0 0.0 copy-done
  31.0 3.3 bitcast_dynamic-update-slice_fusion
  34.4 0.9 fusion.16
  35.2 0.9 fusion.15
  36.1 5.2 constant_dynamic-slice_fusion.1.wqkv
  41.3 9.6 %fusion.4.xn = bf16[12,192,2048]{2,1,0:T(8,128)(2,1)} fusion(bf16[12,192,2048]{2,1,0:T(8,128)(2,1)} %param.7, f32[2048]{0:T(1024)S(1)} %convert_element_type.19, f32[12,192]{1,0:T(8,128)S(1)} %add_rsqrt_fusion), kind=kLoop, calls=%fused_computation.7 | loop fusion | flops 18874368 | bytes 18891776 | tf_op jit(solution)/shard_map/convert_element_type | solution.py:327
  50.9 515.7 %shard_map.126 = (bf16[4,12,192,2048]{3,2,1,0:T(8,128)(2,1)}, bf16[4,12,192,2048]{3,2,1,0:T(8,128)(2,1)}, f32[1024,2048]{1,0:T(8,128)}, f32[1280,2048]{1,0:T(8,1...) custom-call(bf16[12,192,2048]{2,1,0:T(8,128)(2,1)} %fusion.4.xn, bf16[12,192,2048]{2,1,0:T(8,128)(2,1)} %dy.1, ...), custom_call_target="tpu_custom_call" | custom-call | tf_op jit(solution)/shard_map/pallas_call | solution.py:287
  566.6 0.0 all-gather.4.cloned.1.call-update
  566.6 0.0 all-gather.6.cloned.1.call-start
  566.7 0.7 all-gather.6.cloned.1.call-update
  567.4 34.1 %fusion.10 = (f32[2048]{0:T(1024)S(1)}, f32[12,192]{1,0:T(8,128)S(1)}, f32[12,192,2048]{2,1,0:T(8,128)}) fusion(bf16[12,192,2048]{2,1,0:T(8,128)(2,1)} %param.7, f32[12,192]{1,0:T(8,128)S(1)} %add_rsqrt_fusion, f32[2048]{0:T(1024)S(1)} %convert_element_type.19, bf16[12,192,2560]{2,1,0:T(8,128)(2,1)} %get-tuple-element.12, bf16[2048,2560]{1,0:T(8,128)(2,1)} %fusion.15), kind=kOutput, calls=%fused_computation.13 | convolution fusion | flops 24192217088 | bytes 50628608 | tf_op jit(solution)/shard_map/bsf,mf->bsm/dot_general | solution.py:348
  601.4 8.8 %psum.7 = f32[2048]{0:T(1024)} all-reduce(f32[2048]{0:T(1024)S(1)} %get-tuple-element.15), channel_id=1, replica_groups=mesh['dp'=2,'cp'=4] {'cp'}, use_global_device_ids=true, to_apply=%region_3.4 | all-reduce | flops 2048 | bytes 16384 | tf_op jit(solution)/shard_map/psum | solution.py:349
  610.3 17.8 %fusion.9 = bf16[12,192,2048]{2,1,0:T(8,128)(2,1)} fusion(bf16[12,192,2048]{2,1,0:T(8,128)(2,1)} %param.7, bf16[12,192,2048]{2,1,0:T(8,128)(2,1)} %dy.1, f32[12,192,2048]{2,1,0:T(8,128)} %get-tuple-element.25, f32[12,192]{1,0:T(8,128)S(1)} %broadcast_multiply_fusion, f32[2048]{0:T(1024)S(1)} %convert_element_type.19, f32[12,192]{1,0:T(8,128)S(1)} %add_rsqrt_fusion), kind=kLoop, calls=%fused_computation.12 | loop fusion | flops 42467328 | bytes 47212544 | tf_op jit(solution)/shard_map/convert_element_type | solution.py:351
  628.0 26.9 %fusion.12 = bf16[12,192,2048]{2,1,0:T(8,128)(2,1)} fusion(bf16[12,192,2048]{2,1,0:T(8,128)(2,1)} %param.7, bf16[12,192,2048]{2,1,0:T(8,128)(2,1)} %get-tuple-element.11, bf16[2048,2048,1]{1,0,2:T(8,128)(2,1)} %bitcast.49), kind=kOutput, calls=%fused_computation.15 | convolution fusion | flops 19341508608 | bytes 36700160 | tf_op jit(solution)/shard_map/bsf,fm->bsm/dot_general | solution.py:347
  655.0 0.0 all-gather.4.cloned.1.call-done
  655.0 0.0 all-gather.6.cloned.1.call-done
  655.0 3.9 fusion.19
  658.9 11.8 %slice.36 = f32[2,1024,2048]{2,1,0:T(8,128)} slice(f32[2,1280,2048]{2,1,0:T(8,128)} %bitcast.41), slice={[0:2], [0:1024], [0:2048]} | slice | bytes 33554432 | tf_op jit(solution)/shard_map/slice | solution.py:343
  670.7 17.6 %copy.21 = f32[16,128,2048]{1,0,2:T(8,128)} copy(f32[16,128,2048]{2,1,0:T(8,128)} %bitcast.39) | data formatting | bytes 33554432 | tf_op jit(solution)/shard_map/reshape | solution.py:343
  688.3 4.1 copy.27
  692.4 2.3 copy.26
  694.7 11.8 %copy.50 = f32[16,128,2048]{2,1,0:T(8,128)} copy(f32[16,128,2048]{2,1,0:T(8,128)} %bitcast.42) | data formatting | bytes 33554432
  (3 shorter events, 0.0 us)
Async XLA Ops:
  7.2 7.0 copy-start.1
  7.2 9.3 %copy-start.2 = (bf16[2048,2,128]{2,1,0:T(2,128)(2,1)S(1)}, bf16[2048,2,128]{2,1,0:T(2,128)(2,1)}, u32[]{:S(2)}) copy-start(bf16[2048,2,128]{2,1,0:T(2,128)(2,1)} %param.12) | copy-start | bytes 3145732
  7.2 647.8 %all-gather.4.cloned.1.call-start = ((), (), s32[]{:S(2)}) async-start(), calls=%async_computation | async-start | bytes 25165824 | tf_op jit(solution)/shard_map/all_gather | solution.py:340
  7.3 11.5 %slice-start = ((s8[8388608]{0:T(1024)(128)(4,1)}), s8[4194304]{0:T(1024)(128)(4,1)S(1)}, s32[]{:S(2)}) async-start(s8[8388608]{0:T(1024)(128)(4,1)} %bitcast.46), calls=%async_computation.2 | async-start | bytes 8388608
  8.1 10.6 %slice-start.1 = ((s8[8388608]{0:T(1024)(128)(4,1)}), s8[4194304]{0:T(1024)(128)(4,1)S(1)}, s32[]{:S(2)}) async-start(s8[8388608]{0:T(1024)(128)(4,1)} %bitcast.46), calls=%async_computation.3 | async-start | bytes 8388608
  21.0 8.3 %copy-start.3 = (bf16[2048,1,128]{2,1,0:T(2,128)(2,1)S(1)}, bf16[2048,1,128]{2,1,0:T(2,128)(2,1)}, u32[]{:S(2)}) copy-start(bf16[2048,1,128]{2,1,0:T(2,128)(2,1)} %get-tuple-element.24) | copy-start | bytes 1572868
  24.4 5.8 copy-start.4
  24.4 6.7 copy-start
  566.6 88.3 %all-gather.6.cloned.1.call-start = ((), (), s32[]{:S(2)}) async-start(), calls=%async_computation.1 | async-start | bytes 31457280 | tf_op jit(solution)/shard_map/all_gather | solution.py:341
Sparse Core Ops, SparseCore 0:
  566.8 29.9 all-gather.3
  598.3 34.5 all-gather.5

commit v2 on v1

--- a/solution.py
+++ b/solution.py
@@ -24,11 +24,11 @@
     return lax.dot_general(a, b, (((1,), (1,)), ((), ())), preferred_element_type=F32)
 
 
-def group_kernel(xn, dy, wqkv, wo, gx, gy, dwo, dwq, oo, dqo,
-                 xb, yb, wq_v, wo_v, acc_o, acc_q, q_s, do_s, k_s, v_s, kt_s, vt_s,
+def group_kernel(x, dy, gain, wq, wkv, wo, gx, gy, dwo, dwq, oo, dqo, xn,
+                 xb, yb, gain_v, wq_v, wo_v, acc_o, acc_q, q_s, do_s, k_s, v_s, kt_s, vt_s,
                  ot_s, dqt_s, dk_acc, dv_acc, o_n, dq_n,
-                 cs, cr, ds, dr, fs, fr, lsem, wsem, osem, psend, precv, fsem):
-    n_seq, blk, dm = xn.shape
+                 cs, cr, ds, dr, fs, fr, lsem, wsem, osem, psend, precv, fsem, nsem):
+    n_seq, blk, dm = x.shape
     seq = 4 * blk
     n_heads, _, hd = q_s.shape
     qw = n_heads * hd
@@ -103,30 +103,81 @@
                                                     device_id={'cp': pair}, device_id_type=MESH))
         return res
 
-    load_wq = pltpu.make_async_copy(wqkv, wq_v, wsem.at[0])
-    load_wo = pltpu.make_async_copy(wo, wo_v, wsem.at[1])
-    load_wq.start()
-    load_wo.start()
+    kvw = 2 * hd
+    weight_loads = [
+        pltpu.make_async_copy(gain, gain_v, wsem.at[0]),
+        pltpu.make_async_copy(wq.at[:, pl.ds(pl.multiple_of(core * qw, 128), qw)], wq_v.at[:, 0:qw], wsem.at[1]),
+        pltpu.make_async_copy(wkv.at[:, pl.ds(pl.multiple_of(core * kvw, 128), kvw)], wq_v.at[:, qw:qw + kvw], wsem.at[2]),
+        pltpu.make_async_copy(wo.at[pl.ds(pl.multiple_of(core * qw, 128), qw)], wo_v, wsem.at[3]),
+    ]
+
+    def norm_in(s):
+        return pltpu.make_async_copy(x.at[s], yb.at[1, pl.ds(pl.multiple_of((s % 2) * blk, 64), blk)], nsem.at[0, s % 2])
+
+    def norm_out(s):
+        return pltpu.make_async_copy(xb.at[1, pl.ds(pl.multiple_of((s % 2) * blk, 64), blk)], xn.at[s], nsem.at[1, s % 2])
+
+    norm_in(0).start()
+    for copy in weight_loads:
+        copy.start()
 
     barrier = pltpu.get_barrier_semaphore()
     for peer in (pair, across):
         pl.semaphore_signal(barrier, inc=1, device_id={'cp': peer}, device_id_type=MESH)
     pl.semaphore_wait(barrier, 2)
 
-    for s in range(CROSS_AHEAD):
-        for t in range(2):
-            cross_copy(t, s).start()
-            if s < PAIR_AHEAD:
-                pair_copy(t, s).start()
-    for t in range(2):
-        load_own(t, 0).start()
+    cross_copy(1, 0).start()
+    pair_copy(1, 0).start()
+    load_own(1, 0).start()
+    weight_loads[0].wait()
+
+    def send_normed(s):
+        norm_out(s).wait()
+
+        @pl.when(s < CROSS_AHEAD)
+        def _():
+            cross_copy(0, s).start()
+
+        @pl.when(s + 1 < CROSS_AHEAD)
+        def _():
+            cross_copy(1, s + 1).start()
+
+        @pl.when(s < PAIR_AHEAD)
+        def _():
+            pair_copy(0, s).start()
+
+        @pl.when(s + 1 < PAIR_AHEAD)
+        def _():
+            pair_copy(1, s + 1).start()
+
+    def norm_step(s, carry):
+        @pl.when(s + 1 < n_seq)
+        def _():
+            norm_in(s + 1).start()
+        norm_in(s).wait()
+        base = (s % 2) * blk
+        for c in range(blk // 48):
+            rows = pl.ds(pl.multiple_of(base + c * 48, 16), 48)
+            xf = yb[1, rows, :].astype(F32)
+            r = lax.rsqrt(jnp.mean(xf * xf, axis=-1, keepdims=True) + EPS)
+            xb[1, rows, :] = (xf * r * gain_v[...]).astype(BF16)
+        norm_out(s).start()
+
+        @pl.when(s > 0)
+        def _():
+            send_normed(s - 1)
+        return carry
+
+    lax.fori_loop(0, n_seq, norm_step, 0)
+    send_normed(n_seq - 1)
+    load_own(0, 0).start()
     acc_o[...] = jnp.zeros_like(acc_o)
     acc_q[...] = jnp.zeros_like(acc_q)
     for t in range(2):
         pair_arrival(t, 0).wait_recv()
         load_from(t, 0, pair, 1).start()
-    load_wq.wait()
-    load_wo.wait()
+    for copy in weight_loads[1:]:
+        copy.wait()
 
     def project_x(slot, r0):
         rows = pl.ds(pl.multiple_of(r0, 128), half)
@@ -149,34 +200,56 @@
             for part in range(tile // hd):
                 do_s[(n * tile + part * hd) // hd, rows, :] = res[:, part * hd:(part + 1) * hd]
 
-    def head_step(h, carry):
-        hrows = pl.ds(pl.multiple_of(h * hd, hd), hd)
-        for i in range(n_tiles):
+    def heads():
+        units = [(h, i) for h in range(n_heads) for i in range(n_tiles)]
+        state = {}
+
+        def score(u):
+            h, i = units[u]
             nk = (i + 1) * tile
             qi = q_s[h, i * tile:(i + 1) * tile, :]
             doi = do_s[h, i * tile:(i + 1) * tile, :]
-            st = dot_nt(k_s[0:nk, :], qi)
-            key_pos = lax.broadcasted_iota(jnp.int32, (nk, tile), 0)
-            qry_pos = lax.broadcasted_iota(jnp.int32, (nk, tile), 1) + i * tile
-            st = jnp.where(key_pos <= qry_pos, st, -jnp.inf)
+            state[u] = [dot_nt(k_s[0:nk, :], qi), dot_nt(v_s[0:nk, :], doi)]
+
+        def attend(u):
+            h, i = units[u]
+            nk = (i + 1) * tile
+            st, dpt = state[u]
+            key_pos = lax.broadcasted_iota(jnp.int32, (tile, tile), 0)
+            qry_pos = lax.broadcasted_iota(jnp.int32, (tile, tile), 1)
+            edge = jnp.where(key_pos <= qry_pos, st[nk - tile:], -jnp.inf)
+            st = edge if i == 0 else jnp.concatenate([st[:nk - tile], edge], axis=0)
             mx = jnp.max(st, axis=0, keepdims=True)
             p = jnp.exp2(st * c2 - mx * c2)
             inv_l = 1.0 / jnp.sum(p, axis=0, keepdims=True)
             ot = (dot_nn(vt_s[:, 0:nk], p.astype(BF16)) * inv_l).astype(BF16)
-            ot_s[hrows, i * tile:(i + 1) * tile] = ot
-            dot_i = doi.astype(F32).T
-            delta = jnp.sum(dot_i * ot.astype(F32), axis=0, keepdims=True)
-            dpt = dot_nt(v_s[0:nk, :], doi)
+            ot_s[h * hd:(h + 1) * hd, i * tile:(i + 1) * tile] = ot
+            state[u] = [p, inv_l, ot, dpt]
+
+        def grads(u):
+            h, i = units[u]
+            nk = (i + 1) * tile
+            p, inv_l, ot, dpt = state.pop(u)
+            qi = q_s[h, i * tile:(i + 1) * tile, :]
+            doi = do_s[h, i * tile:(i + 1) * tile, :]
+            delta = jnp.sum(doi.astype(F32).T * ot.astype(F32), axis=0, keepdims=True)
             pn = p * inv_l
             dst = (pn * (dpt - delta) * scale).astype(BF16)
             dv_acc[0:nk, :] += dot_nn(pn.astype(BF16), doi)
             dk_acc[0:nk, :] += dot_nn(dst, qi)
-            dqt_s[hrows, i * tile:(i + 1) * tile] = dot_nn(kt_s[:, 0:nk], dst).astype(BF16)
+            dqt_s[h * hd:(h + 1) * hd, i * tile:(i + 1) * tile] = dot_nn(kt_s[:, 0:nk], dst).astype(BF16)
+
+        for t in range(-2, len(units)):
+            if t + 2 < len(units):
+                score(t + 2)
+            if 0 <= t + 1 < len(units):
+                attend(t + 1)
+            if t >= 0:
+                grads(t)
         own_cols = pl.ds(pl.multiple_of(chip * half, 128), half)
-        hcols = pl.ds(pl.multiple_of(h * hd, hd), hd)
-        o_n[:, hcols] = ot_s[hrows, own_cols].T
-        dq_n[:, hcols] = dqt_s[hrows, own_cols].T
-        return carry
+        for h in range(n_heads):
+            o_n[:, h * hd:(h + 1) * hd] = ot_s[h * hd:(h + 1) * hd, own_cols].T
+            dq_n[:, h * hd:(h + 1) * hd] = dqt_s[h * hd:(h + 1) * hd, own_cols].T
 
     def seq_step(s, carry):
         slot = s % 2
@@ -231,7 +304,7 @@
                 local.wait()
                 remote.wait_send()
 
-        lax.fori_loop(0, n_heads, head_step, 0)
+        heads()
 
         near_rows = pl.ds(pl.multiple_of(near, 128), half)
         for idx, acc in enumerate((dk_acc, dv_acc)):
@@ -275,15 +348,17 @@
     flush_q.wait()
 
 
-def group_call(x_norm, dy_in, wqkv, wo):
-    n_seq, blk, dm = x_norm.shape
+def group_call(x_in, dy_in, gain, wq, wkv, wo):
+    n_seq, blk, dm = x_in.shape
     seq = 4 * blk
-    qw = wo.shape[0]
-    hd = (wqkv.shape[1] - qw) // 2
+    qw = wq.shape[1] // 2
+    hd = wkv.shape[1] // 4
     n_heads = qw // hd
-    kw = wqkv.shape[1]
+    kw = qw + 2 * hd
     any_spec = pl.BlockSpec(memory_space=pl.ANY)
     dma = pltpu.SemaphoreType.DMA
+    rows = n_seq * seq
+    flops = 2 * rows * dm * (2 * kw + 2 * qw) + 12 * n_seq * n_heads * seq * seq * hd
     return pl.pallas_call(
         group_kernel,
         out_shape=(
@@ -293,11 +368,12 @@
             jax.ShapeDtypeStruct((kw, dm), F32),
             jax.ShapeDtypeStruct((n_seq, blk, 2 * qw), BF16),
             jax.ShapeDtypeStruct((n_seq, blk, 2 * kw), BF16),
+            jax.ShapeDtypeStruct((n_seq, blk, dm), BF16),
         ),
-        in_specs=[any_spec] * 4,
-        out_specs=(any_spec,) * 6,
+        in_specs=[any_spec] * 6,
+        out_specs=(any_spec,) * 7,
         scratch_shapes=[
-            pltpu.VMEM((2, seq, dm), BF16), pltpu.VMEM((2, seq, dm), BF16),
+            pltpu.VMEM((2, seq, dm), BF16), pltpu.VMEM((2, seq, dm), BF16), pltpu.VMEM((1, dm), F32),
             pltpu.VMEM((dm, kw), BF16), pltpu.VMEM((qw, dm), BF16),
             pltpu.VMEM((qw, dm), F32), pltpu.VMEM((kw, dm), F32),
             pltpu.VMEM((n_heads, seq, hd), BF16), pltpu.VMEM((n_heads, seq, hd), BF16),
@@ -307,49 +383,165 @@
             pltpu.VMEM((seq, hd), F32), pltpu.VMEM((seq, hd), F32),
             pltpu.VMEM((2 * blk, qw), BF16), pltpu.VMEM((2 * blk, kw), BF16),
             dma((2, n_seq)), dma((2, n_seq)), dma((2, n_seq)), dma((2, n_seq)), dma((2, n_seq)), dma((2, n_seq)),
-            dma((2, 4)), dma((2,)), dma((2,)), dma((2,)), dma((2, n_seq)), dma((2,)),
+            dma((2, 4)), dma((4,)), dma((2,)), dma((2,)), dma((2, n_seq)), dma((2,)), dma((2, 2)),
         ],
+        cost_estimate=pl.CostEstimate(flops=flops, bytes_accessed=400_000_000, transcendentals=0),
         compiler_params=pltpu.CompilerParams(collective_id=0, has_side_effects=True, vmem_limit_bytes=67_000_000),
-    )(x_norm, dy_in, wqkv, wo)
+    )(x_in, dy_in, gain, wq, wkv, wo)
+
+
+def dx_kernel(dq, w_all, x, dy, gain, dx, dg, dn):
+    i = pl.program_id(0)
+    n_tiles = pl.num_programs(0) - 1
+    tm, dm = x.shape
+    parts = 4
+    cw = dm // parts
+    cr = tm // parts
+
+    def matmul(n):
+        cols = pl.ds(pl.multiple_of(n * cw, cw), cw)
+        dn[i % 2, :, cols] = dot_nt(dq[...], w_all[cols, :])
+
+    def finish(n):
+        rows = pl.ds(pl.multiple_of(n * cr, 16), cr)
+        xf = x[rows, :].astype(F32)
+        r = lax.rsqrt(jnp.mean(xf * xf, axis=-1, keepdims=True) + EPS)
+        u = xf * r
+        d = dn[(i + 1) % 2, rows, :]
+        du = d * u
+        dg[...] += jnp.sum(du.reshape(cr // 8, 8, dm), axis=0)
+        g = gain[...]
+        mean_eu = jnp.mean(du * g, axis=-1, keepdims=True)
+        dx[rows, :] = (dy[rows, :].astype(F32) + r * (d * g - u * mean_eu)).astype(BF16)
+
+    @pl.when(i == 0)
+    def _():
+        dg[...] = jnp.zeros_like(dg)
+
+        @pl.loop(0, parts)
+        def _(n):
+            matmul(n)
+
+    @pl.when(jnp.logical_and(i > 0, i < n_tiles))
+    def _():
+        @pl.loop(0, parts)
+        def _(n):
+            finish(n)
+            matmul(n)
+
+    @pl.when(i == n_tiles)
+    def _():
+        @pl.loop(0, parts)
+        def _(n):
+            finish(n)
+
+
+def dx_call(dq, w_all, x, dy, gain):
+    rows, dm = x.shape
+    kw = dq.shape[1]
+    tm = 384
+    n_tiles = rows // tm
+    late = lambda i: (jnp.maximum(i - 1, 0), 0)
+    return pl.pallas_call(
+        dx_kernel,
+        grid=(n_tiles + 1,),
+        out_shape=(jax.ShapeDtypeStruct((rows, dm), BF16), jax.ShapeDtypeStruct((8, dm), F32)),
+        in_specs=[pl.BlockSpec((tm, kw), lambda i: (jnp.minimum(i, n_tiles - 1), 0)),
+                  pl.BlockSpec((dm, kw), lambda i: (0, 0)),
+                  pl.BlockSpec((tm, dm), late), pl.BlockSpec((tm, dm), late),
+                  pl.BlockSpec((1, dm), lambda i: (0, 0))],
+        out_specs=(pl.BlockSpec((tm, dm), late), pl.BlockSpec((8, dm), lambda i: (0, 0))),
+        scratch_shapes=[pltpu.VMEM((2, tm, dm), F32)],
+        cost_estimate=pl.CostEstimate(flops=2 * rows * dm * kw, bytes_accessed=50_000_000, transcendentals=0),
+        compiler_params=pltpu.CompilerParams(vmem_limit_bytes=60_000_000),
+    )(dq, w_all, x, dy, gain)
+
+
+def y_kernel(core_ref, o, wo, x, own_o, recv_o, own_q, recv_q, y, d_wo, d_wq, d_wk, d_wv):
+    i = pl.program_id(0)
+    core = core_ref[0]
+    n_heads, hd = d_wq.shape[1], d_wq.shape[2]
+    n_group = n_heads // 2
+    y[...] = (x[...].astype(F32) + dot_nn(o[...], wo[...])).astype(BF16)
+    mine = i // (pl.num_programs(0) // 2) == core
+    d_wo[...] = jnp.where(mine, own_o[...], recv_o[...])
+    for g in range(2):
+        own = core == g
+        for h in range(n_group + 2):
+            rows = pl.ds(h * hd, hd)
+            val = jnp.where(own, own_q[rows, :], recv_q[rows, :]).T
+            if h < n_group:
+                d_wq[:, g * n_group + h, :] = val
+            elif h == n_group:
+                d_wk[:, g, :] = val
+            else:
+                d_wv[:, g, :] = val
+
+
+def y_call(core, o, wo, x, own_o, recv_o, own_q, recv_q, n_heads, hd):
+    rows, dm = x.shape
+    qw2 = o.shape[1]
+    kw = own_q.shape[0]
+    steps = 8
+    tm = rows // steps
+    tw = qw2 // steps
+    tn = dm // steps
+    hs = steps // 2
+    grid_spec = pltpu.PrefetchScalarGridSpec(
+        num_scalar_prefetch=1,
+        grid=(steps,),
+        in_specs=[pl.BlockSpec((tm, qw2), lambda i, c: (i, 0)),
+                  pl.BlockSpec((qw2, dm), lambda i, c: (0, 0)),
+                  pl.BlockSpec((tm, dm), lambda i, c: (i, 0)),
+                  pl.BlockSpec((tw, dm), lambda i, c: (jnp.clip(i - hs * c[0], 0, hs - 1), 0)),
+                  pl.BlockSpec((tw, dm), lambda i, c: (jnp.clip(i - hs * (1 - c[0]), 0, hs - 1), 0)),
+                  pl.BlockSpec((kw, tn), lambda i, c: (0, i)),
+                  pl.BlockSpec((kw, tn), lambda i, c: (0, i))],
+        out_specs=(pl.BlockSpec((tm, dm), lambda i, c: (i, 0)),
+                   pl.BlockSpec((tw, dm), lambda i, c: (i, 0)),
+                   pl.BlockSpec((tn, n_heads, hd), lambda i, c: (i, 0, 0)),
+                   pl.BlockSpec((tn, 2, hd), lambda i, c: (i, 0, 0)),
+                   pl.BlockSpec((tn, 2, hd), lambda i, c: (i, 0, 0))))
+    return pl.pallas_call(
+        y_kernel,
+        grid_spec=grid_spec,
+        out_shape=(jax.ShapeDtypeStruct((rows, dm), BF16), jax.ShapeDtypeStruct((qw2, dm), F32),
+                   jax.ShapeDtypeStruct((dm, n_heads, hd), F32),
+                   jax.ShapeDtypeStruct((dm, 2, hd), F32), jax.ShapeDtypeStruct((dm, 2, hd), F32)),
+        cost_estimate=pl.CostEstimate(flops=2 * rows * dm * qw2, bytes_accessed=110_000_000, transcendentals=0),
+        compiler_params=pltpu.CompilerParams(vmem_limit_bytes=60_000_000),
+    )(core, o, wo, x, own_o, recv_o, own_q, recv_q)
 
 
 def solution(mesh):
     def device_fn(x_in, dy_in, norm_gain, w_q, w_k, w_v, w_o):
         n_batch, blk, dm = x_in.shape
         n_heads, hd = w_q.shape[1], w_q.shape[2]
-        kv_heads = w_k.shape[1]
-        n_group = n_heads // kv_heads
-        core = lax.axis_index('cp') % 2
-        gain = norm_gain.astype(F32)
-        x_f32 = x_in.astype(F32)
-        inv_rms = lax.rsqrt(jnp.mean(x_f32 * x_f32, axis=-1, keepdims=True) + EPS)
-        unit = x_f32 * inv_rms
-        x_norm = (unit * gain).astype(BF16)
-
-        w_all = jnp.concatenate(
-            [part for g in range(kv_heads) for part in
-             (w_q[:, g * n_group:(g + 1) * n_group].reshape(dm, n_group * hd), w_k[:, g], w_v[:, g])], axis=1)
-        kw = w_all.shape[1] // kv_heads
-        wqkv = lax.dynamic_slice(w_all, (0, core * kw), (dm, kw))
-        wo_all = w_o.reshape(n_heads * hd, dm)
-        wo = lax.dynamic_slice(wo_all, (core * n_group * hd, 0), (n_group * hd, dm))
-
-        _, _, dwo_half, dwq_half, o_own, dq_own = group_call(x_norm, dy_in, wqkv, wo)
-
-        pairs = [[0, 1], [2, 3]]
-        d_wo = lax.all_gather(dwo_half, 'cp', axis_index_groups=pairs, tiled=True).reshape(n_heads, hd, dm)
-        dwq_all = lax.all_gather(dwq_half, 'cp', axis_index_groups=pairs)
-        qw = n_group * hd
-        d_wq = dwq_all[:, :qw].reshape(n_heads, hd, dm).transpose(2, 0, 1)
-        d_wk = dwq_all[:, qw:qw + hd].transpose(2, 0, 1)
-        d_wv = dwq_all[:, qw + hd:].transpose(2, 0, 1)
-
-        y_out = (x_f32 + jnp.einsum('bsf,fm->bsm', o_own, wo_all, preferred_element_type=F32)).astype(BF16)
-        d_norm = jnp.einsum('bsf,mf->bsm', dq_own, w_all, preferred_element_type=F32)
-        d_gain = lax.psum(jnp.sum(d_norm * unit, axis=(0, 1)), 'cp')
-        d_unit = d_norm * gain
-        dx_out = (dy_in.astype(F32) + inv_rms * (d_unit - unit * jnp.mean(d_unit * unit, axis=-1, keepdims=True))).astype(BF16)
-        return y_out, dx_out, d_gain, d_wq, d_wk, d_wv, d_wo
+        rows = n_batch * blk
+        qw = n_heads * hd // 2
+        core = (lax.axis_index('cp') % 2).astype(jnp.int32).reshape(1)
+        gain = norm_gain.astype(F32).reshape(1, dm)
+        wq = w_q.reshape(dm, n_heads * hd)
+        wkv = jnp.concatenate([w_k, w_v], axis=2).reshape(dm, 4 * hd)
+        wo = w_o.reshape(n_heads * hd, dm)
+
+        _, _, dwo_own, dwq_own, o_own, dq_own, _ = group_call(x_in, dy_in, gain, wq, wkv, wo)
+
+        n_dev = mesh.shape['cp']
+        pair_perm = [(d, d ^ 1) for d in range(n_dev)]
+        dwo_recv, dwq_recv = lax.ppermute((dwo_own, dwq_own), 'cp', pair_perm)
+
+        w_all = jnp.concatenate([wq[:, :qw], wkv[:, :2 * hd], wq[:, qw:], wkv[:, 2 * hd:]], axis=1)
+        x2 = x_in.reshape(rows, dm)
+        dx, dg = dx_call(dq_own.reshape(rows, -1), w_all, x2, dy_in.reshape(rows, dm), gain)
+        dg = jnp.sum(dg, axis=0)
+        dg1 = lax.ppermute(dg, 'cp', pair_perm)
+        dg2 = lax.ppermute(dg, 'cp', [(d, d ^ 2) for d in range(n_dev)])
+        dg3 = lax.ppermute(dg, 'cp', [(d, d ^ 3) for d in range(n_dev)])
+        d_gain = (dg + dg1) + (dg2 + dg3)
+        y, d_wo, d_wq, d_wk, d_wv = y_call(core, o_own.reshape(rows, -1), wo, x2, dwo_own, dwo_recv, dwq_own, dwq_recv,
+                                           n_heads, hd)
+        return (y.reshape(x_in.shape), dx.reshape(x_in.shape), d_gain, d_wq, d_wk, d_wv, d_wo.reshape(n_heads, hd, dm))
 
     act_spec = P('dp', 'cp', None)
     mat_spec = P(None, None, None)

time: 715 us -> 571 us (0.80)
  matrix products: 61 us -> 0 us
  local copies, waits for them, and re-layouts: 78.7 us -> 18.5 us
  other arithmetic: 34.3 us -> 13.7 us
  Pallas kernels: 516 us -> 531 us
  between operations: 14.1 us -> 0.82 us
  blocking collectives: 8.81 us -> 0 us
    pallas_call x0 -> x2, Pallas kernels: none -> 85.5 us  [the longest x1 45.2 us: y_call(): pl.pallas_call(y_kernel, grid_spec=grid_spec, out_shape=(jax.ShapeDtypeSt...]
    pallas_call x1, Pallas kernels: 516 us -> 446 us  [group_call(): pl.pallas_call(group_kernel, out_shape=(jax.ShapeDtypeStruct((4, n_seq, b...]
    dot_general x2 -> x0, matrix products: 61 us -> none  [the longest x1 34.1 us: device_fn(): jnp.einsum('bsf,mf->bsm', dq_own, w_all, preferred_element_type=F32)]
    convert_element_type x3 -> x0, other arithmetic: 28.3 us -> none  [the longest x1 17.8 us: device_fn(): (dy_in.astype(F32) + inv_rms * (d_unit - unit * jnp.mean(d_unit * unit, a...]
    reshape x1 -> x0, local copies, waits for them, and re-layouts: 17.6 us -> none  [device_fn(): d_wq = dwq_all[:, :qw].reshape(n_heads, hd, dm).transpose(2, 0, 1)]
    slice x5 -> x2, local copies, waits for them, and re-layouts: 22.6 us -> 5.61 us  [the longest x1 3.94 us: device_fn(): wq[:, :qw]]
    unnamed x22 -> x6, local copies, waits for them, and re-layouts: 27.5 us -> 12.9 us
    concatenate x0 -> x2, other arithmetic: none -> 10.8 us  [the longest x1 8.55 us: device_fn(): jnp.concatenate([wq[:, :qw], wkv[:, :2 * hd], wq[:, qw:], wkv[:, 2 * hd:]...]
  transfers between devices with their start and end apart: 2 -> 5, of which waited for: 0 -> 2; matrix products, arithmetic and copies ran while one was open for 11% -> 3% of each run, Pallas kernels for 0% -> 7%
where the time goes in v2:
time: 571 us; the launch traced here: 570 us
  Pallas kernels  531 us (93%)
  local copies, waits for them, and re-layouts  18.5 us (3%)
  other arithmetic  13.7 us (2%)
    pallas_call x1, Pallas kernels, group_call(): pl.pallas_call(group_kernel, out_shape=(jax.ShapeDtypeStruct((4, n_seq, b...  446 us
    pallas_call x1, Pallas kernels, y_call(): pl.pallas_call(y_kernel, grid_spec=grid_spec, out_shape=(jax.ShapeDtypeSt...  45.2 us
    pallas_call x1, Pallas kernels, dx_call(): pl.pallas_call(dx_kernel, grid=(n_tiles + 1,), out_shape=(jax.ShapeDtypeS...  40.3 us
    unnamed x6, local copies, waits for them, and re-layouts  12.9 us
  transfers between devices with their start and end apart: 5, of which 2 were waited for; matrix products, arithmetic and copies ran while one was open for 3% of the time, Pallas kernels for 7%

profile of v2, /device:TPU:0, one launch (start us, length us, event | category | flops | bytes accessed | tf_op | source)
XLA Modules:
  0.0 569.5 jit_solution(2958406839753477978)
XLA Ops:
  0.6 0.0 copy-start
  0.6 0.0 copy-start.1
  0.7 1.4 reshape.65
  2.1 11.1 %copy.17 = bf16[256,8,16,128]{3,1,2,0:T(8,128)(2,1)} copy(bf16[256,8,16,128]{3,2,1,0:T(8,128)(2,1)} %bitcast.18) | data formatting | bytes 16777216
  13.1 0.0 copy-done
  13.1 0.0 copy-done.1
  13.1 2.3 pad_maximum_fusion.1
  15.4 1.8 copy.15
  17.3 445.6 %shard_map.126 = (bf16[4,12,192,2048]{3,2,1,0:T(8,128)(2,1)}, bf16[4,12,192,2048]{3,2,1,0:T(8,128)(2,1)}, f32[1024,2048]{1,0:T(8,128)}, f32[1280,2048]{1,0:T(8,1...) custom-call(bf16[12,192,2048]{2,1,0:T(8,128)(2,1)} %x.1, ...), custom_call_target="tpu_custom_call" | custom-call | flops 260919263232 | bytes 400000000 | tf_op jit(solution)/shard_map/pallas_call | solution.py:362
  462.8 0.3 collective-permute-start.1
  463.2 0.2 collective-permute-start
  463.4 1.7 fusion.1
  465.1 3.9 fusion
  469.0 8.6 %pad_maximum_fusion.w_all = bf16[2048,2560]{1,0:T(8,128)(2,1)} fusion(bf16[2048,256]{1,0:T(8,128)(2,1)S(1)} %get-tuple-element.32, bf16[2048,1024]{1,0:T(8,128)(2,1)S(1)} %get-tuple-element.30, bf16[2048,256]{1,0:T(8,128)(2,1)S(1)} %get-tuple-element.31, bf16[2048,1024]{1,0:T(8,128)(2,1)S(1)} %get-tuple-element.29), kind=kLoop, calls=%fused_computation | loop fusion | flops 41943040 | bytes 20971520 | tf_op jit(solution)/shard_map/concatenate | solution.py:534
  477.6 40.3 %shard_map.128 = (bf16[2304,2048]{1,0:T(8,128)(2,1)}, f32[8,2048]{1,0:T(8,128)}) custom-call(bf16[2304,2560]{1,0:T(8,128)(2,1)} %bitcast.30, bf16[2048,2560]{1,0:T(8,128)(2,1)} %pad_maximum_fusion.w_all, bf16[2304,2048]{1,0:T(8,128)(2,1)} %bitcast.25, bf16[2304,2048]{1,0:T(8,128)(2,1)} %bitcast.24, f32[1,2048]{1,0:T(1,128)} %bitcast.23), custom_call_target="tpu_custom_call" | custom-call | flops 24159191040 | bytes 50000000 | tf_op jit(solution)/shard_map/pallas_call | solution.py:445
  517.8 0.9 reduce_sum.9
  518.7 1.8 collective-permute-start.3
  520.5 0.0 collective-permute-start.4
  520.5 0.4 collective-permute-start.2
  520.9 1.5 collective-permute-done.3
  522.4 1.2 collective-permute-done.4
  523.6 0.0 collective-permute-done.2
  523.6 0.6 add_add_fusion
  524.2 0.0 collective-permute-done.recv_o
  524.2 0.0 collective-permute-done.1.recv_q
  524.2 45.2 %shard_map.127 = (bf16[2304,2048]{1,0:T(8,128)(2,1)}, f32[2048,2048]{1,0:T(8,128)}, f32[2048,16,128]{2,1,0:T(8,128)}, f32[2048,2,128]{2,1,0:T(2,128)}, f32[2048,2,128]{2,1,0:T(2,128)}) custom-call(s32[1]{0:T(128)} %bitcast.core_ref, bf16[2304,2048]{1,0:T(8,128)(2,1)} %bitcast.31, bf16[2048,2048]{1,0:T(8,128)(2,1)} %bitcast.28, bf16[2304,2048]{1,0:T(8,128)(2,1)} %bitcast.26, ...), custom_call_target="tpu_custom_call" | custom-call | flops 19327352832 | bytes 110000000 | tf_op jit(solution)/shard_map/pallas_call | solution.py:505
Async XLA Ops:
  0.6 12.5 %copy-start = (bf16[2048,2,128]{2,1,0:T(2,128)(2,1)S(1)}, bf16[2048,2,128]{2,1,0:T(2,128)(2,1)}, u32[]{:S(2)}) copy-start(bf16[2048,2,128]{2,1,0:T(2,128)(2,1)} %param.12) | copy-start | bytes 3145732
  0.6 12.5 %copy-start.1 = (bf16[2048,2,128]{2,1,0:T(2,128)(2,1)S(1)}, bf16[2048,2,128]{2,1,0:T(2,128)(2,1)}, u32[]{:S(2)}) copy-start(bf16[2048,2,128]{2,1,0:T(2,128)(2,1)} %param.11) | copy-start | bytes 3145732
  462.8 61.3 %collective-permute-start.1 = (f32[1280,2048]{1,0:T(8,128)}, f32[1280,2048]{1,0:T(8,128)}, u32[]{:S(2)}, u32[]{:S(2)}) collective-permute-start(f32[1280,2048]{1,0:T(8,128)} %get-tuple-element.20.own_q), channel_id=1, source_target_pairs={{0,1},{1,0},{2,3},{3,2},{4,5},{5,4},{6,7},{7,6}} | collective-permute-start | bytes 31457288 | tf_op jit(solution)/shard_map/ppermute | solution.py:532
  463.2 61.0 %collective-permute-start = (f32[1024,2048]{1,0:T(8,128)}, f32[1024,2048]{1,0:T(8,128)}, u32[]{:S(2)}, u32[]{:S(2)}) collective-permute-start(f32[1024,2048]{1,0:T(8,128)} %get-tuple-element.19.own_o), channel_id=1, source_target_pairs={{0,1},{1,0},{2,3},{3,2},{4,5},{5,4},{6,7},{7,6}} | collective-permute-start | bytes 25165832 | tf_op jit(solution)/shard_map/ppermute | solution.py:532
  518.7 3.7 collective-permute-start.3
  520.5 3.1 collective-permute-start.4
  520.5 3.1 collective-permute-start.2

commit v3 on v2

--- a/solution.py
+++ b/solution.py
@@ -24,10 +24,10 @@
     return lax.dot_general(a, b, (((1,), (1,)), ((), ())), preferred_element_type=F32)
 
 
-def group_kernel(x, dy, gain, wq, wkv, wo, gx, gy, dwo, dwq, oo, dqo, xn,
-                 xb, yb, gain_v, wq_v, wo_v, acc_o, acc_q, q_s, do_s, k_s, v_s, kt_s, vt_s,
+def group_kernel(x, dy, gain, w_q, wkv, wo, gx, gy, dwo, dwq, oo, dqo, xn, wq,
+                 xb, yb, gain_v, w_in, w_f32, wq_v, wo_v, acc_o, acc_q, q_s, do_s, k_s, v_s, kt_s, vt_s,
                  ot_s, dqt_s, dk_acc, dv_acc, o_n, dq_n,
-                 cs, cr, ds, dr, fs, fr, lsem, wsem, osem, psend, precv, fsem, nsem):
+                 cs, cr, ds, dr, fs, fr, lsem, wsem, osem, psend, precv, fsem, nsem, rsem):
     n_seq, blk, dm = x.shape
     seq = 4 * blk
     n_heads, _, hd = q_s.shape
@@ -81,29 +81,28 @@
     def load_from(t, s, b, j):
         return pltpu.make_async_copy(land_of[t].at[b, s], vmem_of[t].at[s % 2, rows_of(b)], lsem.at[t, j])
 
+    kvw = 2 * hd
+
+    def out_parts(s, g):
+        q_cols = pl.ds(pl.multiple_of(g * qw, 128), qw)
+        kv_cols = pl.ds(pl.multiple_of(2 * qw + g * kvw, 128), kvw)
+        return ((o_n, slice(0, qw), oo.at[s, :, q_cols]),
+                (dq_n, slice(0, qw), dqo.at[s, :, q_cols]),
+                (dq_n, slice(qw, qw + kvw), dqo.at[s, :, kv_cols]))
+
+    def pair_send(idx, s, buf, cols, dst):
+        rows = pl.ds(pl.multiple_of((1 - core) * blk, 64), blk)
+        return pltpu.make_async_remote_copy(buf.at[rows, cols], dst, psend.at[idx], precv.at[idx, s],
+                                            device_id={'cp': pair}, device_id_type=MESH)
+
     def out_copies(s):
-        own_rows = pl.ds(pl.multiple_of(core * blk, 64), blk)
-        pair_rows = pl.ds(pl.multiple_of((1 - core) * blk, 64), blk)
-        res = []
-        for idx, (buf, out) in enumerate(((o_n, oo), (dq_n, dqo))):
-            width = buf.shape[1]
-            cols = pl.ds(pl.multiple_of(core * width, 128), width)
-            res.append((pltpu.make_async_copy(buf.at[own_rows], out.at[s, :, cols], osem.at[idx]),
-                        pltpu.make_async_remote_copy(buf.at[pair_rows], out.at[s, :, cols], psend.at[idx], precv.at[idx, s],
-                                                     device_id={'cp': pair}, device_id_type=MESH)))
-        return res
+        rows = pl.ds(pl.multiple_of(core * blk, 64), blk)
+        return [(pltpu.make_async_copy(buf.at[rows, cols], dst, osem.at[idx]), pair_send(idx, s, buf, cols, dst))
+                for idx, (buf, cols, dst) in enumerate(out_parts(s, core))]
 
     def out_arrivals(s):
-        pair_rows = pl.ds(pl.multiple_of((1 - core) * blk, 64), blk)
-        res = []
-        for idx, (buf, out) in enumerate(((o_n, oo), (dq_n, dqo))):
-            width = buf.shape[1]
-            cols = pl.ds(pl.multiple_of((1 - core) * width, 128), width)
-            res.append(pltpu.make_async_remote_copy(buf.at[pair_rows], out.at[s, :, cols], psend.at[idx], precv.at[idx, s],
-                                                    device_id={'cp': pair}, device_id_type=MESH))
-        return res
-
-    kvw = 2 * hd
+        return [pair_send(idx, s, buf, cols, dst) for idx, (buf, cols, dst) in enumerate(out_parts(s, 1 - core))]
+
     weight_loads = [
         pltpu.make_async_copy(gain, gain_v, wsem.at[0]),
         pltpu.make_async_copy(wq.at[:, pl.ds(pl.multiple_of(core * qw, 128), qw)], wq_v.at[:, 0:qw], wsem.at[1]),
@@ -117,8 +116,37 @@
     def norm_out(s):
         return pltpu.make_async_copy(xb.at[1, pl.ds(pl.multiple_of((s % 2) * blk, 64), blk)], xn.at[s], nsem.at[1, s % 2])
 
+    n_wrows = w_in.shape[1]
+    n_wsteps = dm // n_wrows
+    stage0 = half
+
+    def relay_in(c):
+        return pltpu.make_async_copy(w_q.at[pl.ds(pl.multiple_of(c * n_wrows, n_wrows), n_wrows)], w_in.at[c % 2],
+                                     rsem.at[0, c % 2])
+
+    def relay_out(c):
+        return pltpu.make_async_copy(xb.at[1, pl.ds(pl.multiple_of(stage0 + (c % 2) * n_wrows, n_wrows), n_wrows)],
+                                     wq.at[pl.ds(pl.multiple_of(c * n_wrows, n_wrows), n_wrows)], rsem.at[1, c % 2])
+
+    def relay_step(c, carry):
+        @pl.when(c + 1 < n_wsteps)
+        def _():
+            relay_in(c + 1).start()
+        relay_in(c).wait()
+
+        @pl.when(c > 1)
+        def _():
+            relay_out(c - 2).wait()
+        w_f32[...] = w_in[c % 2].astype(F32)
+        rows = pl.ds(pl.multiple_of(stage0 + (c % 2) * n_wrows, n_wrows), n_wrows)
+        for h in range(2 * n_heads):
+            xb[1, rows, h * hd:(h + 1) * hd] = w_f32[:, h, :].astype(BF16)
+        relay_out(c).start()
+        return carry
+
     norm_in(0).start()
-    for copy in weight_loads:
+    relay_in(0).start()
+    for copy in (weight_loads[0], weight_loads[2], weight_loads[3]):
         copy.start()
 
     barrier = pltpu.get_barrier_semaphore()
@@ -171,6 +199,10 @@
     lax.fori_loop(0, n_seq, norm_step, 0)
     send_normed(n_seq - 1)
     load_own(0, 0).start()
+    lax.fori_loop(0, n_wsteps, relay_step, 0)
+    relay_out(n_wsteps - 2).wait()
+    relay_out(n_wsteps - 1).wait()
+    weight_loads[1].start()
     acc_o[...] = jnp.zeros_like(acc_o)
     acc_q[...] = jnp.zeros_like(acc_q)
     for t in range(2):
@@ -315,21 +347,37 @@
             local.start()
             remote.start()
 
-        def dw_step(n, c):
+        def dwo_step(n, c):
             cols = pl.ds(pl.multiple_of(n * 2 * tile, 2 * tile), 2 * tile)
             acc_o[:, cols] += dot_nn(ot_s[...], yb[slot, :, cols])
+            return c
+
+        lax.fori_loop(0, dm // (2 * tile), dwo_step, 0)
+
+        @pl.when(s == n_seq - 1)
+        def _():
+            flush_o.start()
+
+        def dwq_step(n, c):
+            cols = pl.ds(pl.multiple_of(n * 2 * tile, 2 * tile), 2 * tile)
             acc_q[:, cols] += dot_nn(dqt_s[...], xb[slot, :, cols])
+
+            @pl.when(s == n_seq - 1)
+            def _():
+                flush_q(n).start()
             return c
 
-        lax.fori_loop(0, dm // (2 * tile), dw_step, 0)
+        lax.fori_loop(0, dm // (2 * tile), dwq_step, 0)
         return carry
 
+    flush_o = pltpu.make_async_copy(acc_o, dwo, fsem.at[0])
+
+    def flush_q(n):
+        cols = pl.ds(pl.multiple_of(n * 2 * tile, 2 * tile), 2 * tile)
+        return pltpu.make_async_copy(acc_q.at[:, cols], dwq.at[:, cols], fsem.at[1 + n])
+
     lax.fori_loop(0, n_seq, seq_step, 0)
 
-    flush_o = pltpu.make_async_copy(acc_o, dwo, fsem.at[0])
-    flush_q = pltpu.make_async_copy(acc_q, dwq, fsem.at[1])
-    flush_o.start()
-    flush_q.start()
     for local, remote in out_copies(n_seq - 1):
         local.wait()
         remote.wait_send()
@@ -345,15 +393,15 @@
 
     lax.fori_loop(0, n_seq, drain, 0)
     flush_o.wait()
-    flush_q.wait()
-
-
-def group_call(x_in, dy_in, gain, wq, wkv, wo):
+    for n in range(dm // (2 * tile)):
+        flush_q(n).wait()
+
+
+def group_call(x_in, dy_in, gain, w_q, wkv, wo):
     n_seq, blk, dm = x_in.shape
     seq = 4 * blk
-    qw = wq.shape[1] // 2
-    hd = wkv.shape[1] // 4
-    n_heads = qw // hd
+    n_heads, hd = w_q.shape[1] // 2, w_q.shape[2]
+    qw = n_heads * hd
     kw = qw + 2 * hd
     any_spec = pl.BlockSpec(memory_space=pl.ANY)
     dma = pltpu.SemaphoreType.DMA
@@ -369,11 +417,13 @@
             jax.ShapeDtypeStruct((n_seq, blk, 2 * qw), BF16),
             jax.ShapeDtypeStruct((n_seq, blk, 2 * kw), BF16),
             jax.ShapeDtypeStruct((n_seq, blk, dm), BF16),
+            jax.ShapeDtypeStruct((dm, 2 * qw), BF16),
         ),
         in_specs=[any_spec] * 6,
-        out_specs=(any_spec,) * 7,
+        out_specs=(any_spec,) * 8,
         scratch_shapes=[
             pltpu.VMEM((2, seq, dm), BF16), pltpu.VMEM((2, seq, dm), BF16), pltpu.VMEM((1, dm), F32),
+            pltpu.VMEM((2, 64, 2 * n_heads, hd), BF16), pltpu.VMEM((64, 2 * n_heads, hd), F32),
             pltpu.VMEM((dm, kw), BF16), pltpu.VMEM((qw, dm), BF16),
             pltpu.VMEM((qw, dm), F32), pltpu.VMEM((kw, dm), F32),
             pltpu.VMEM((n_heads, seq, hd), BF16), pltpu.VMEM((n_heads, seq, hd), BF16),
@@ -383,14 +433,14 @@
             pltpu.VMEM((seq, hd), F32), pltpu.VMEM((seq, hd), F32),
             pltpu.VMEM((2 * blk, qw), BF16), pltpu.VMEM((2 * blk, kw), BF16),
             dma((2, n_seq)), dma((2, n_seq)), dma((2, n_seq)), dma((2, n_seq)), dma((2, n_seq)), dma((2, n_seq)),
-            dma((2, 4)), dma((4,)), dma((2,)), dma((2,)), dma((2, n_seq)), dma((2,)), dma((2, 2)),
+            dma((2, 4)), dma((4,)), dma((3,)), dma((3,)), dma((3, n_seq)), dma((1 + dm // 512,)), dma((2, 2)), dma((2, 2)),
         ],
         cost_estimate=pl.CostEstimate(flops=flops, bytes_accessed=400_000_000, transcendentals=0),
         compiler_params=pltpu.CompilerParams(collective_id=0, has_side_effects=True, vmem_limit_bytes=67_000_000),
-    )(x_in, dy_in, gain, wq, wkv, wo)
-
-
-def dx_kernel(dq, w_all, x, dy, gain, dx, dg, dn):
+    )(x_in, dy_in, gain, w_q, wkv, wo)
+
+
+def dx_kernel(dq, wq, wkv, x, dy, gain, dx, dg, dn, w_all, wsem):
     i = pl.program_id(0)
     n_tiles = pl.num_programs(0) - 1
     tm, dm = x.shape
@@ -416,10 +466,22 @@
 
     @pl.when(i == 0)
     def _():
+        qw = wq.shape[1]
+
+        def loads(n):
+            rows = pl.ds(pl.multiple_of(n * cw, cw), cw)
+            return (pltpu.make_async_copy(wq.at[rows], w_all.at[rows, 0:qw], wsem.at[0, n]),
+                    pltpu.make_async_copy(wkv.at[rows], w_all.at[rows, qw:], wsem.at[1, n]))
+
+        for n in range(parts):
+            for copy in loads(n):
+                copy.start()
         dg[...] = jnp.zeros_like(dg)
 
         @pl.loop(0, parts)
         def _(n):
+            for copy in loads(n):
+                copy.wait()
             matmul(n)
 
     @pl.when(jnp.logical_and(i > 0, i < n_tiles))
@@ -436,46 +498,64 @@
             finish(n)
 
 
-def dx_call(dq, w_all, x, dy, gain):
+def dx_call(dq, wq, wkv, x, dy, gain):
     rows, dm = x.shape
     kw = dq.shape[1]
     tm = 384
     n_tiles = rows // tm
     late = lambda i: (jnp.maximum(i - 1, 0), 0)
+    any_spec = pl.BlockSpec(memory_space=pl.ANY)
     return pl.pallas_call(
         dx_kernel,
         grid=(n_tiles + 1,),
         out_shape=(jax.ShapeDtypeStruct((rows, dm), BF16), jax.ShapeDtypeStruct((8, dm), F32)),
         in_specs=[pl.BlockSpec((tm, kw), lambda i: (jnp.minimum(i, n_tiles - 1), 0)),
-                  pl.BlockSpec((dm, kw), lambda i: (0, 0)),
+                  any_spec, any_spec,
                   pl.BlockSpec((tm, dm), late), pl.BlockSpec((tm, dm), late),
                   pl.BlockSpec((1, dm), lambda i: (0, 0))],
         out_specs=(pl.BlockSpec((tm, dm), late), pl.BlockSpec((8, dm), lambda i: (0, 0))),
-        scratch_shapes=[pltpu.VMEM((2, tm, dm), F32)],
+        scratch_shapes=[pltpu.VMEM((2, tm, dm), F32), pltpu.VMEM((dm, kw), BF16), pltpu.SemaphoreType.DMA((2, 4))],
         cost_estimate=pl.CostEstimate(flops=2 * rows * dm * kw, bytes_accessed=50_000_000, transcendentals=0),
         compiler_params=pltpu.CompilerParams(vmem_limit_bytes=60_000_000),
-    )(dq, w_all, x, dy, gain)
-
-
-def y_kernel(core_ref, o, wo, x, own_o, recv_o, own_q, recv_q, y, d_wo, d_wq, d_wk, d_wv):
+    )(dq, wq, wkv, x, dy, gain)
+
+
+def y_kernel(core_ref, o, wo, x, own_o, recv_o, own_q, recv_q, y, d_wo, d_wq, d_wk, d_wv, wo_v, wsem):
     i = pl.program_id(0)
     core = core_ref[0]
     n_heads, hd = d_wq.shape[1], d_wq.shape[2]
     n_group = n_heads // 2
-    y[...] = (x[...].astype(F32) + dot_nn(o[...], wo[...])).astype(BF16)
-    mine = i // (pl.num_programs(0) // 2) == core
-    d_wo[...] = jnp.where(mine, own_o[...], recv_o[...])
-    for g in range(2):
-        own = core == g
-        for h in range(n_group + 2):
-            rows = pl.ds(h * hd, hd)
-            val = jnp.where(own, own_q[rows, :], recv_q[rows, :]).T
-            if h < n_group:
-                d_wq[:, g * n_group + h, :] = val
-            elif h == n_group:
-                d_wk[:, g, :] = val
-            else:
-                d_wv[:, g, :] = val
+    load = pltpu.make_async_copy(wo, wo_v, wsem)
+
+    def place():
+        mine = i // (pl.num_programs(0) // 2) == core
+        d_wo[...] = jnp.where(mine, own_o[...], recv_o[...])
+        for g in range(2):
+            own = core == g
+            for h in range(n_group + 2):
+                rows = pl.ds(h * hd, hd)
+                val = jnp.where(own, own_q[rows, :], recv_q[rows, :]).T
+                if h < n_group:
+                    d_wq[:, g * n_group + h, :] = val
+                elif h == n_group:
+                    d_wk[:, g, :] = val
+                else:
+                    d_wv[:, g, :] = val
+
+    def project():
+        y[...] = (x[...].astype(F32) + dot_nn(o[...], wo_v[...])).astype(BF16)
+
+    @pl.when(i == 0)
+    def _():
+        load.start()
+        place()
+        load.wait()
+        project()
+
+    @pl.when(i > 0)
+    def _():
+        project()
+        place()
 
 
 def y_call(core, o, wo, x, own_o, recv_o, own_q, recv_q, n_heads, hd):
@@ -491,7 +571,7 @@
         num_scalar_prefetch=1,
         grid=(steps,),
         in_specs=[pl.BlockSpec((tm, qw2), lambda i, c: (i, 0)),
-                  pl.BlockSpec((qw2, dm), lambda i, c: (0, 0)),
+                  pl.BlockSpec(memory_space=pl.ANY),
                   pl.BlockSpec((tm, dm), lambda i, c: (i, 0)),
                   pl.BlockSpec((tw, dm), lambda i, c: (jnp.clip(i - hs * c[0], 0, hs - 1), 0)),
                   pl.BlockSpec((tw, dm), lambda i, c: (jnp.clip(i - hs * (1 - c[0]), 0, hs - 1), 0)),
@@ -501,7 +581,8 @@
                    pl.BlockSpec((tw, dm), lambda i, c: (i, 0)),
                    pl.BlockSpec((tn, n_heads, hd), lambda i, c: (i, 0, 0)),
                    pl.BlockSpec((tn, 2, hd), lambda i, c: (i, 0, 0)),
-                   pl.BlockSpec((tn, 2, hd), lambda i, c: (i, 0, 0))))
+                   pl.BlockSpec((tn, 2, hd), lambda i, c: (i, 0, 0))),
+        scratch_shapes=[pltpu.VMEM((qw2, dm), BF16), pltpu.SemaphoreType.DMA])
     return pl.pallas_call(
         y_kernel,
         grid_spec=grid_spec,
@@ -521,26 +602,25 @@
         qw = n_heads * hd // 2
         core = (lax.axis_index('cp') % 2).astype(jnp.int32).reshape(1)
         gain = norm_gain.astype(F32).reshape(1, dm)
-        wq = w_q.reshape(dm, n_heads * hd)
         wkv = jnp.concatenate([w_k, w_v], axis=2).reshape(dm, 4 * hd)
         wo = w_o.reshape(n_heads * hd, dm)
 
-        _, _, dwo_own, dwq_own, o_own, dq_own, _ = group_call(x_in, dy_in, gain, wq, wkv, wo)
+        _, _, dwo_own, dwq_own, o_own, dq_own, _, wq = group_call(x_in, dy_in, gain, w_q, wkv, wo)
 
         n_dev = mesh.shape['cp']
         pair_perm = [(d, d ^ 1) for d in range(n_dev)]
         dwo_recv, dwq_recv = lax.ppermute((dwo_own, dwq_own), 'cp', pair_perm)
 
-        w_all = jnp.concatenate([wq[:, :qw], wkv[:, :2 * hd], wq[:, qw:], wkv[:, 2 * hd:]], axis=1)
         x2 = x_in.reshape(rows, dm)
-        dx, dg = dx_call(dq_own.reshape(rows, -1), w_all, x2, dy_in.reshape(rows, dm), gain)
+        dx, dg = dx_call(dq_own.reshape(rows, -1), wq, wkv, x2, dy_in.reshape(rows, dm), gain)
         dg = jnp.sum(dg, axis=0)
         dg1 = lax.ppermute(dg, 'cp', pair_perm)
         dg2 = lax.ppermute(dg, 'cp', [(d, d ^ 2) for d in range(n_dev)])
         dg3 = lax.ppermute(dg, 'cp', [(d, d ^ 3) for d in range(n_dev)])
-        d_gain = (dg + dg1) + (dg2 + dg3)
         y, d_wo, d_wq, d_wk, d_wv = y_call(core, o_own.reshape(rows, -1), wo, x2, dwo_own, dwo_recv, dwq_own, dwq_recv,
                                            n_heads, hd)
+        y, dg, dg1, dg2, dg3 = lax.optimization_barrier((y, dg, dg1, dg2, dg3))
+        d_gain = (dg + dg1) + (dg2 + dg3)
         return (y.reshape(x_in.shape), dx.reshape(x_in.shape), d_gain, d_wq, d_wk, d_wv, d_wo.reshape(n_heads, hd, dm))
 
     act_spec = P('dp', 'cp', None)

time: 571 us -> 552 us (0.967)
  local copies, waits for them, and re-layouts: 18.5 us -> 1.77 us
  other arithmetic: 13.7 us -> 6.54 us
  Pallas kernels: 531 us -> 538 us
    unnamed x6 -> x1, local copies, waits for them, and re-layouts: 12.9 us -> 1.77 us
    concatenate x1 -> x0, other arithmetic: 8.55 us -> none  [device_fn(): jnp.concatenate([wq[:, :qw], wkv[:, :2 * hd], wq[:, qw:], wkv[:, 2 * hd:]...]
    pallas_call x1, Pallas kernels: 446 us -> 452 us  [group_call(): pl.pallas_call(group_kernel, out_shape=(jax.ShapeDtypeStruct((4, n_seq, b...]
  transfers between devices with their start and end apart: 5 -> 5, of which waited for: 2 -> 0; matrix products, arithmetic and copies ran while one was open for 3% -> 0% of each run, Pallas kernels for 7% -> 16%
where the time goes in v3:
time: 552 us; the launch traced here: 550 us
  Pallas kernels  538 us (97%)
  other arithmetic  6.54 us (1%)
    pallas_call x1, Pallas kernels, group_call(): pl.pallas_call(group_kernel, out_shape=(jax.ShapeDtypeStruct((4, n_seq, b...  452 us
    pallas_call x1, Pallas kernels, y_call(): pl.pallas_call(y_kernel, grid_spec=grid_spec, out_shape=(jax.ShapeDtypeSt...  45.3 us
    pallas_call x1, Pallas kernels, dx_call(): pl.pallas_call(dx_kernel, grid=(n_tiles + 1,), out_shape=(jax.ShapeDtypeS...  40 us
  transfers between devices with their start and end apart: 5, of which 0 were waited for; matrix products, arithmetic and copies ran while one was open for 0% of the time, Pallas kernels for 16%

profile of v3, /device:TPU:0, one launch (start us, length us, event | category | flops | bytes accessed | tf_op | source)
XLA Modules:
  0.0 549.6 jit_solution(14277236366736932712)
XLA Ops:
  0.6 1.3 reshape.61
  1.9 3.8 pad_maximum_fusion
  5.7 1.8 copy.14
  7.5 452.2 %shard_map.126 = (bf16[4,12,192,2048]{3,2,1,0:T(8,128)(2,1)}, bf16[4,12,192,2048]{3,2,1,0:T(8,128)(2,1)}, f32[1024,2048]{1,0:T(8,128)}, f32[1280,2048]{1,0:T(8,1...) custom-call(bf16[12,192,2048]{2,1,0:T(8,128)(2,1)} %x.1, ...), custom_call_target="tpu_custom_call" | custom-call | flops 260919263232 | bytes 400000000 | tf_op jit(solution)/shard_map/pallas_call | solution.py:410
  459.7 0.2 collective-permute-start.1
  459.9 0.4 collective-permute-start
  460.2 40.0 %shard_map.128 = (bf16[2304,2048]{1,0:T(8,128)(2,1)}, f32[8,2048]{1,0:T(8,128)}) custom-call(bf16[2304,2560]{1,0:T(8,128)(2,1)} %bitcast.23, bf16[2048,2048]{1,0:T(8,128)(2,1)} %get-tuple-element.29.wq, bf16[2048,512]{1,0:T(8,128)(2,1)} %bitcast.14, bf16[2304,2048]{1,0:T(8,128)(2,1)} %bitcast.18, bf16[2304,2048]{1,0:T(8,128)(2,1)} %bitcast.17, ...), custom_call_target="tpu_custom_call" | custom-call | flops 24159191040 | bytes 50000000 | tf_op jit(solution)/shard_map/pallas_call | solution.py:508
  500.2 0.9 reduce_sum.9
  501.1 2.2 collective-permute-start.4
  503.3 0.3 collective-permute-start.3
  503.5 0.1 collective-permute-start.2
  503.6 0.0 collective-permute-done.recv_o
  503.6 0.0 collective-permute-done.1.recv_q
  503.6 45.3 %shard_map.127 = (bf16[2304,2048]{1,0:T(8,128)(2,1)}, f32[2048,2048]{1,0:T(8,128)}, f32[2048,16,128]{2,1,0:T(8,128)}, f32[2048,2,128]{2,1,0:T(2,128)}, f32[2048,2,128]{2,1,0:T(2,128)}) custom-call(s32[1]{0:T(128)} %bitcast.core_ref, bf16[2304,2048]{1,0:T(8,128)(2,1)} %bitcast.25, bf16[2048,2048]{1,0:T(8,128)(2,1)} %bitcast.21, bf16[2304,2048]{1,0:T(8,128)(2,1)} %bitcast.19, ...), custom_call_target="tpu_custom_call" | custom-call | flops 19327352832 | bytes 110000000 | tf_op jit(solution)/shard_map/pallas_call | solution.py:586
  549.0 0.0 collective-permute-done.4
  549.0 0.0 collective-permute-done.3
  549.0 0.0 collective-permute-done.2
  549.0 0.6 add_add_fusion
Async XLA Ops:
  459.7 43.9 %collective-permute-start.1 = (f32[1280,2048]{1,0:T(8,128)}, f32[1280,2048]{1,0:T(8,128)}, u32[]{:S(2)}, u32[]{:S(2)}) collective-permute-start(f32[1280,2048]{1,0:T(8,128)} %get-tuple-element.26.own_q), channel_id=1, source_target_pairs={{0,1},{1,0},{2,3},{3,2},{4,5},{5,4},{6,7},{7,6}} | collective-permute-start | bytes 31457288 | tf_op jit(solution)/shard_map/ppermute | solution.py:612
  459.9 43.7 %collective-permute-start = (f32[1024,2048]{1,0:T(8,128)}, f32[1024,2048]{1,0:T(8,128)}, u32[]{:S(2)}, u32[]{:S(2)}) collective-permute-start(f32[1024,2048]{1,0:T(8,128)} %get-tuple-element.25.own_o), channel_id=1, source_target_pairs={{0,1},{1,0},{2,3},{3,2},{4,5},{5,4},{6,7},{7,6}} | collective-permute-start | bytes 25165832 | tf_op jit(solution)/shard_map/ppermute | solution.py:612
  501.1 47.9 %collective-permute-start.4 = (f32[2048]{0:T(1024)S(1)}, f32[2048]{0:T(1024)S(1)}, u32[]{:S(2)}, u32[]{:S(2)}) collective-permute-start(f32[2048]{0:T(1024)S(1)} %reduce_sum.9), channel_id=1, source_target_pairs={{0,3},{1,2},{2,1},{3,0},{4,7},{5,6},{6,5},{7,4}} | collective-permute-start | bytes 24584 | tf_op jit(solution)/shard_map/ppermute | solution.py:619
  503.3 45.7 %collective-permute-start.3 = (f32[2048]{0:T(1024)S(1)}, f32[2048]{0:T(1024)S(1)}, u32[]{:S(2)}, u32[]{:S(2)}) collective-permute-start(f32[2048]{0:T(1024)S(1)} %reduce_sum.9), channel_id=1, source_target_pairs={{0,2},{1,3},{2,0},{3,1},{4,6},{5,7},{6,4},{7,5}} | collective-permute-start | bytes 24584 | tf_op jit(solution)/shard_map/ppermute | solution.py:618
  503.5 45.5 %collective-permute-start.2 = (f32[2048]{0:T(1024)S(1)}, f32[2048]{0:T(1024)S(1)}, u32[]{:S(2)}, u32[]{:S(2)}) collective-permute-start(f32[2048]{0:T(1024)S(1)} %reduce_sum.9), channel_id=1, source_target_pairs={{0,1},{1,0},{2,3},{3,2},{4,5},{5,4},{6,7},{7,6}} | collective-permute-start | bytes 24584 | tf_op jit(solution)/shard_map/ppermute | solution.py:617
